TPU v7x, 128 devices: a whole 4x4x4 slice. The times are simulated.
128 devices in a mesh: dp: 32 (over z, y, core), tensor: 4 (over x).
Axes of the slice: x: 4, y: 4, z: 4, core: 2. Of those that a mesh axis runs over, the one named last changes fastest.
Arguments:
- tokens: bfloat16 [12288, 2880], P('dp', 'tensor'), may hold values from -6 to 6
- out_grad: bfloat16 [12288, 2880], P('dp', 'tensor'), may hold values from -6 to 6
- route_probs: bfloat16 [12288, 4], P('dp'), may hold values from 0.099609375 to 1
- expert_ids: int32 [12288, 4], P('dp'), may hold values from 0 to 127, all different within a row; in each aligned block of 384 rows (0 to 383, 384 to 767, ...) at most 18 rows name the same one
- placement_map: int32 [128], replicated, may hold values from 0 to 127, each once
- w_gate: bfloat16 [32, 2880, 2880], P('dp', None, 'tensor'), may hold values from -0.109375 to 0.109375
- w_up: bfloat16 [32, 2880, 2880], P('dp', None, 'tensor'), may hold values from -0.109375 to 0.109375
- w_down: bfloat16 [32, 2880, 2880], P('dp', 'tensor'), may hold values from -0.109375 to 0.109375
Outputs:
- input_grad: bfloat16 [12288, 2880], P('dp', 'tensor')
- gate_grad: bfloat16 [32, 2880, 2880], P('dp', None, 'tensor')
- up_grad: bfloat16 [32, 2880, 2880], P('dp', None, 'tensor')
- down_grad: bfloat16 [32, 2880, 2880], P('dp', 'tensor')
- prob_grad: bfloat16 [12288, 4], P('dp')
Inputs may be any that keep to these rules, and one draw needn't show every extreme that they name: `expert_ids`: each row names 4 different experts. In the rows of one index of dp no expert is named by more than 18 rows, a bound that some block reaches. `placement_map`: A permutation: every value is taken by exactly one expert.
All inputs are finite; a program needn't handle non-finite values.
Results may differ from a plain program's by a relative error of at most 0.011.
Values may be sent and summed in bfloat16 or wider, within the bound.
No kernel may reach another device: no remote copies, remote signals or barrier semaphores. Data moves between devices by JAX's collectives and lax.ppermute only.
A program may use at most 128 MiB of HBM per device.

v0:
```python
import jax
import jax.numpy as jnp
from jax import lax
from jax.experimental import pallas as pl
from jax.experimental.pallas import tpu as pltpu
from jax.sharding import PartitionSpec as P


SWISH_SLOPE = 1.702
EXP_OWN = 4
OWNERS = 32
CAP = 18
MAIN = 16
ROWS = OWNERS * CAP
MROWS = OWNERS * MAIN
TOK = 384
TOP = 4
WID = 720
PAD = 768
FEAT = 2880
FPAD = 2944
SIDES = 4
GATE_VMEM = 58
BACK_VMEM = 55
PROB = 720

BF = jnp.bfloat16
F32 = jnp.float32
NT = (((1,), (1,)), ((), ()))
TN = (((0,), (0,)), ((), ()))
NN = (((1,), (0,)), ((), ()))


def dot(a, b, dims):
    return lax.dot_general(a, b, dims, preferred_element_type=F32)


def call(body, out_shape, **kw):
    params = pltpu.CompilerParams(vmem_limit_bytes=kw.pop("vmem", 8) << 20, **({"dimension_semantics": ("arbitrary",)} if "grid" in kw else {}))
    flops = kw.pop("flops", 0)
    nbytes = kw.pop("nbytes", 4 << 20)
    return pl.pallas_call(
        body,
        out_shape=out_shape,
        compiler_params=params,
        cost_estimate=pl.CostEstimate(flops=flops, bytes_accessed=nbytes, transcendentals=0),
        **kw,
    )


def struct(shape, dtype=BF):
    return jax.ShapeDtypeStruct(shape, dtype)


def vm():
    return pl.BlockSpec(memory_space=pltpu.VMEM)


def sm():
    return pl.BlockSpec(memory_space=pltpu.SMEM)


def iota(shape, dim):
    return lax.broadcasted_iota(jnp.int32, shape, dim)


def swap_matrix():
    r, q = iota((128, 128), 0), iota((128, 128), 1)
    return (((r >> 4) == ((q >> 1) & 7)) & ((q >> 4) == ((r >> 1) & 7)) & ((r & 1) == (q & 1))).astype(BF)


def tiles_of(width):
    return width // 128


def block_rows(width):
    t = tiles_of(width)
    return MAIN * t + 16 * ((t + 7) // 8)


def pack_rest(rest, out_ref, width):
    t = tiles_of(width)
    swap = swap_matrix()
    for a in range((t + 7) // 8):
        for i in range(OWNERS // 8):
            parts = [
                rest[16 * i : 16 * i + 16, 128 * j : 128 * j + 128] if j < t else jnp.zeros((16, 128), BF)
                for j in range(8 * a, 8 * a + 8)
            ]
            turned = dot(swap, jnp.concatenate(parts, axis=0), NN).astype(BF)
            out_ref[8 * i : 8 * i + 8, MAIN * t + 16 * a : MAIN * t + 16 * a + 16, :] = turned.reshape(8, 16, 128)


def unpack(ref, width, store, first=0):
    t = tiles_of(width)
    peers = ref.shape[0]
    for j in range(t):
        store(MAIN * first, 128 * j, ref[:, MAIN * j : MAIN * j + MAIN, :].reshape(MAIN * peers, 128))
    swap = swap_matrix()
    for a in range((t + 7) // 8):
        for i in range(peers // 8):
            block = ref[8 * i : 8 * i + 8, MAIN * t + 16 * a : MAIN * t + 16 * a + 16, :].reshape(128, 128)
            turned = dot(swap, block, NN).astype(BF)
            for b in range(8):
                j = 8 * a + b
                if j < t:
                    store(MROWS + 2 * first + 16 * i, 128 * j, turned[16 * b : 16 * b + 16])


def row_owner(shape, dim):
    r = iota(shape, dim)
    return jnp.where(r < MROWS, r >> 4, (r - MROWS) >> 1)


def row_slot(shape, dim):
    r = iota(shape, dim)
    return jnp.where(r < MROWS, r & 15, MAIN + (r & 1))


def hits_of(ids_ref, map_ref):
    experts = map_ref.shape[1]
    eq = map_ref[...] == EXP_OWN * iota((OWNERS, experts), 0)
    held = jnp.sum(jnp.where(eq, iota((OWNERS, experts), 1), 0), axis=1, keepdims=True)
    return [ids_ref[k : k + 1, :] == held for k in range(TOP)]


def dispatch_x_body(ids_ref, prob_ref, map_ref, tok_ref, send_ref, pick_ref, tokp, rest):
    hits = hits_of(ids_ref, map_ref)
    probs = prob_ref[...].astype(F32)
    named = hits[0] | hits[1] | hits[2] | hits[3]
    p_on = jnp.zeros((OWNERS, TOK), F32)
    for k in range(TOP):
        p_on = jnp.where(hits[k], probs[k : k + 1, :], p_on)
    upper = (iota((TOK, TOK), 0) < iota((TOK, TOK), 1)).astype(F32).astype(BF)
    rank = dot(named.astype(F32).astype(BF), upper, NN)
    key = jnp.where(named, rank, -1.0).astype(BF)
    spread = (row_owner((ROWS, OWNERS), 0) == iota((ROWS, OWNERS), 1)).astype(F32).astype(BF)
    pick = dot(spread, key, NN) == row_slot((ROWS, TOK), 0).astype(F32)
    p_col = jnp.sum(jnp.where(pick, dot(spread, p_on.astype(BF), NN), 0.0), axis=1, keepdims=True)
    pick = pick.astype(F32).astype(BF)
    pick_ref[...] = pick
    tokp[0:WID, :] = tok_ref[...]
    tokp[WID:PAD, :] = jnp.zeros((PAD - WID, TOK), BF)
    for q in range(3):
        val = dot(pick, tokp[256 * q : 256 * q + 256, :], NT)
        if q == 2:
            val = jnp.where(iota((ROWS, 256), 1) == PROB - 512, p_col, val)
        val = val.astype(BF)
        for j in (2 * q, 2 * q + 1):
            tile = val[:, 128 * (j - 2 * q) : 128 * (j - 2 * q) + 128]
            send_ref[:, MAIN * j : MAIN * j + MAIN, :] = tile[:MROWS].reshape(OWNERS, MAIN, 128)
            rest[:, 128 * j : 128 * j + 128] = tile[MROWS:]
    pack_rest(rest, send_ref, PAD)


def dispatch_d_body(t_ref, pick_ref, own_ref, below_ref, above_ref, far_a_ref, far_b_ref, send_ref, full, rest):
    t = t_ref[0]

    def put(side, ref, off, rows):
        j = lax.rem(t + side, SIDES)
        full[pl.ds(pl.multiple_of(WID * j + off, 16), rows), :] = ref[...]

    put(0, own_ref, 0, WID)
    put(3, below_ref, 0, WID)
    put(1, above_ref, 0, WID)
    put(2, far_a_ref, 0, 368)
    put(2, far_b_ref, 368, WID - 368)
    full[FEAT:3072, :] = jnp.zeros((3072 - FEAT, TOK), BF)
    pick = pick_ref[...]
    for q in range(12):
        val = dot(pick, full[256 * q : 256 * q + 256, :], NT).astype(BF)
        for j in (2 * q, 2 * q + 1):
            if j < tiles_of(FPAD):
                tile = val[:, 128 * (j - 2 * q) : 128 * (j - 2 * q) + 128]
                send_ref[:, MAIN * j : MAIN * j + MAIN, :] = tile[:MROWS].reshape(OWNERS, MAIN, 128)
                rest[:, 128 * j : 128 * j + 128] = tile[MROWS:]
    pack_rest(rest, send_ref, FPAD)


def turn_body(t_ref, w_ref, out_ref):
    t = t_ref[0]
    pieces = [w_ref[:, WID * j : WID * j + WID] for j in range(SIDES)]
    for k in range(SIDES):
        j = lax.rem(t + k, SIDES)
        piece = jnp.where(j == 0, pieces[0], jnp.where(j == 1, pieces[1], jnp.where(j == 2, pieces[2], pieces[3])))
        out_ref[k, :, 0:WID] = piece
        out_ref[k, :, WID:PAD] = jnp.zeros((piece.shape[0], PAD - WID), BF)


CHUNKS = ((0, 256), (256, 256), (512, WID - 512))


def copies(pairs, sems):
    out = []
    for n, (src, dst) in enumerate(pairs):
        copy = pltpu.make_async_copy(src, dst, sems.at[n])
        copy.start()
        out.append(copy)
    return out


def gate_up_body(*refs):
    x_refs, w_refs, (act_out, mid_out, x_out), (w, act, mid, x, in_sems, out_sems) = refs[:7], refs[7:9], refs[9:12], refs[12:]
    loads = copies(
        [(w_refs[n].at[:, lo : lo + size, :], w.at[n, :, lo : lo + size, :]) for lo, size in CHUNKS for n in range(2)], in_sems
    )

    def keep(side):
        def store(row, lane, value):
            x[side, row : row + value.shape[0], lane : lane + 128] = value

        return store

    unpack(x_refs[0], PAD, keep(0))
    for n, side in enumerate((3, 1, 2)):
        unpack(x_refs[2 * n + 1], PAD, keep(side), 0)
        unpack(x_refs[2 * n + 2], PAD, keep(side), OWNERS // 2)
    stores = [pltpu.make_async_copy(x, x_out, out_sems.at[6])]
    stores[0].start()
    for c, (lo, size) in enumerate(CHUNKS):
        loads[2 * c].wait()
        loads[2 * c + 1].wait()
        gate, up1 = (sum(dot(x[k], w[n, k, lo : lo + size, :], NT) for k in range(SIDES)) for n in range(2))
        up1 = up1 + 1.0
        sig = 1.0 / (1.0 + jnp.exp(-SWISH_SLOPE * gate))
        glu = gate * sig
        act[:, lo : lo + size] = (glu * up1).astype(BF)
        mid[0, :, lo : lo + size] = up1 * (sig + SWISH_SLOPE * glu * (1.0 - sig))
        mid[1, :, lo : lo + size] = glu
        if c == 2:
            tile = x[0, :, 640:768].astype(F32)
            p_col = jnp.sum(jnp.where(iota((ROWS, 128), 1) == PROB - 640, tile, 0.0), axis=1, keepdims=True)
            mid[0, :, WID:PAD] = jnp.broadcast_to(p_col, (ROWS, PAD - WID))
            mid[1, :, WID:PAD] = jnp.zeros((ROWS, PAD - WID), F32)
            act[:, WID:PAD] = jnp.zeros((ROWS, PAD - WID), BF)
        cols = slice(lo, lo + 256)
        for n, (src, dst) in enumerate(((act.at[:, cols], act_out.at[:, cols]), (mid.at[:, :, cols], mid_out.at[:, :, cols]))):
            stores.append(pltpu.make_async_copy(src, dst, out_sems.at[2 * c + n]))
            stores[-1].start()
    for copy in stores:
        copy.wait()


def back_body(
    got_hbm, wd_hbm, act_hbm, mid_hbm, wg_hbm, wu_hbm,
    d_out, gg_ref, gu_ref, prob_ref, p_ref, a_ref, b_ref,
    got, wd, act, mid, wg, wu, d, sems, out_sem,
):
    got_loads = copies([(got_hbm.at[8 * i : 8 * i + 8], got.at[8 * i : 8 * i + 8]) for i in range(4)], sems)
    loads = copies(
        [(wd_hbm.at[lo : lo + size, :], wd.at[lo : lo + size, :]) for lo, size in CHUNKS]
        + [(mid_hbm, mid), (act_hbm, act), (wg_hbm.at[2], wg), (wu_hbm.at[2], wu)],
        sems.at[4:],
    )

    def store(row, lane, value):
        width = min(128, FEAT - lane)
        d[row : row + value.shape[0], lane : lane + width] = value[:, :width]

    for i in range(4):
        got_loads[i].wait()
        unpack(got.at[8 * i : 8 * i + 8], FPAD, store, 8 * i)
    keep_d = pltpu.make_async_copy(d, d_out, out_sem)
    keep_d.start()
    total = jnp.zeros((ROWS, 1), F32)
    for c, (lo, size) in enumerate(CHUNKS):
        loads[c].wait()
        down_back = dot(d[...], wd[lo : lo + size, :], NT)
        if c == 0:
            loads[3].wait()
            loads[4].wait()
            p_col = mid[0, :, 640:768][:, WID - 640 : WID - 639]
            p_ref[...] = p_col
        delta = p_col * down_back
        gg_ref[:, lo : lo + size] = (delta * mid[0, :, lo : lo + size]).astype(BF)
        gu_ref[:, lo : lo + size] = (delta * mid[1, :, lo : lo + size]).astype(BF)
        total = total + jnp.sum(act[:, lo : lo + size].astype(F32) * down_back, axis=1, keepdims=True)
    prob_ref[...] = jnp.where(iota((ROWS, 128), 1) == PROB - 640, total, 0.0)
    loads[5].wait()
    loads[6].wait()
    left, right = dx_of(gg_ref[...], gu_ref[...], wg[...], wu[...], prob_ref[...])
    right = split_prob(right)
    put_rows(a_ref, left[:HALF], right[:HALF])
    put_rows(b_ref, left[HALF:], right[HALF:])
    keep_d.wait()


def split_prob(tile):
    lane = iota(tile.shape, 1)
    total = jnp.sum(jnp.where(lane == PROB - 640, tile, 0.0), axis=1, keepdims=True)
    high = total.astype(BF).astype(F32)
    return jnp.where(lane == PROB - 640, high, jnp.where(lane == PROB - 639, total - high, tile))


def join_prob(tile):
    lane = iota(tile.shape, 1)
    total = jnp.sum(jnp.where((lane == PROB - 640) | (lane == PROB - 639), tile, 0.0), axis=1, keepdims=True)
    return jnp.where(lane == PROB - 640, total, jnp.where(lane == PROB - 639, 0.0, tile))


HALF = ROWS // 2


def dx_of(gg, gu, wg, wu, prob):
    val = dot(gg, wg, NN) + dot(gu, wu, NN)
    return val[:, :640], val[:, 640:768] + prob


def put_rows(ref, left, right):
    ref[:, 0:640] = left.astype(ref.dtype)
    ref[:, 640:768] = right.astype(ref.dtype)


def near_dx_body(gg_ref, gu_ref, wga_ref, wua_ref, wgb_ref, wub_ref, prob_ref, send_a, send_b, keep_a, keep_b):
    gg, gu, prob = gg_ref[...], gu_ref[...], prob_ref[...]
    left, right = dx_of(gg, gu, wga_ref[0], wua_ref[0], prob)
    put_rows(send_a, left[HALF:], split_prob(right)[HALF:])
    put_rows(keep_a, left[:HALF], right[:HALF])
    left, right = dx_of(gg, gu, wgb_ref[0], wub_ref[0], prob)
    put_rows(send_b, left[:HALF], split_prob(right)[:HALF])
    put_rows(keep_b, left[HALF:], right[HALF:])


def own_dx_body(gg_ref, gu_ref, wg_ref, wu_ref, prob_ref, out_ref):
    put_rows(out_ref, *dx_of(gg_ref[...], gu_ref[...], wg_ref[0], wu_ref[0], prob_ref[...]))


def relay_body(keep_a, came_a, keep_b, came_b, out_a, out_b):
    for keep, came, out in ((keep_a, came_a, out_a), (keep_b, came_b, out_b)):
        left = keep[:, 0:640] + came[:, 0:640].astype(F32)
        put_rows(out, left, split_prob(keep[:, 640:768] + join_prob(came[:, 640:768].astype(F32))))


def sum_body(own_ref, below_a, below_b, above_a, above_b, send_ref, rest):
    for j in range(tiles_of(PAD)):
        cols = slice(128 * j, 128 * j + 128)
        tile = [
            own_ref[lo : lo + HALF, cols] + below[:, cols].astype(F32) + above[:, cols].astype(F32)
            for lo, below, above in ((0, below_a, above_a), (HALF, below_b, above_b))
        ]
        tile = jnp.concatenate(tile, axis=0)
        if j == 5:
            tile = join_prob(tile)
        tile = tile.astype(BF)
        send_ref[:, MAIN * j : MAIN * j + MAIN, :] = tile[:MROWS].reshape(OWNERS, MAIN, 128)
        rest[:, cols] = tile[MROWS:]
    pack_rest(rest, send_ref, PAD)


def combine_body(back_ref, pick_ref, ids_ref, map_ref, dx_ref, dp_ref, rows):
    def store(row, lane, value):
        rows[row : row + value.shape[0], lane : lane + 128] = value

    unpack(back_ref, PAD, store)
    pick = pick_ref[...]
    dx_ref[...] = dot(rows[...], pick, TN)[:WID].astype(BF)
    tile = rows[:, 640:768].astype(F32)
    p_col = jnp.sum(jnp.where(iota((ROWS, 128), 1) == PROB - 640, tile, 0.0), axis=1, keepdims=True)
    spread = (row_owner((OWNERS, ROWS), 1) == iota((OWNERS, ROWS), 0)).astype(F32).astype(BF)
    per_owner = dot(spread, (pick.astype(F32) * p_col).astype(BF), NN)
    hits = hits_of(ids_ref, map_ref)
    for k in range(TOP):
        dp_ref[k : k + 1, :] = jnp.sum(jnp.where(hits[k], per_owner, 0.0), axis=0, keepdims=True).astype(BF)


def grad_pair_body(t_ref, x_ref, gg_ref, gu_ref, gate_ref, up_ref):
    t = t_ref[0]
    for j in range(SIDES):
        k = lax.rem(j - t + SIDES, SIDES)
        x = x_ref[pl.ds(k, 1)][0]
        for src, out in ((gg_ref, gate_ref), (gu_ref, up_ref)):
            out[:, WID * j : WID * j + WID] = dot(src[...], x, TN).astype(BF)[:, :WID]


def down_body(d_ref, act_ref, p_ref, out_ref, scaled):
    @pl.when(pl.program_id(0) == 0)
    def _():
        scaled[...] = (d_ref[...].astype(F32) * p_ref[...]).astype(BF)

    out_ref[...] = dot(act_ref[...], scaled[...], TN).astype(BF)


def turn(w, t):
    return call(
        turn_body,
        struct((SIDES, WID, PAD)),
        grid=(3,),
        in_specs=[sm(), pl.BlockSpec((240, FEAT), lambda i: (i, 0))],
        out_specs=pl.BlockSpec((SIDES, 240, PAD), lambda i: (0, i, 0)),
        vmem=60,
    )(t, w)


def hbm():
    return pl.BlockSpec(memory_space=pltpu.HBM)


def dma(*shape):
    return pltpu.SemaphoreType.DMA(shape)


def whole(shape):
    return pl.BlockSpec(shape, lambda i: (0,) * len(shape))


def hold(*values):
    return lax.optimization_barrier(values)


def shards(tokens, out_grad, route_probs, expert_ids, placement_map, w_gate, w_up, w_down):
    above = [((i + 1) % SIDES, i) for i in range(SIDES)]
    below = [((i - 1) % SIDES, i) for i in range(SIDES)]

    def from_above(value):
        return lax.ppermute(value, "tensor", above)

    def from_below(value):
        return lax.ppermute(value, "tensor", below)

    t = lax.axis_index("tensor").astype(jnp.int32).reshape(1)
    tok_t, d_t, ids_t, prob_t = tokens.T, out_grad.T, expert_ids.T, route_probs.T
    pmap = placement_map.reshape(1, -1)
    wg_t, wu_t, wd = w_gate[0].T, w_up[0].T, w_down[0]
    bx = block_rows(PAD)
    bd = block_rows(FPAD)
    t, d_t = hold(t, d_t)
    d_above, d_below = from_above(d_t), from_below(d_t)
    send_x, pick = call(
        dispatch_x_body,
        (struct((OWNERS, bx, 128)), struct((ROWS, TOK))),
        in_specs=[vm()] * 4,
        out_specs=(vm(), vm()),
        scratch_shapes=[pltpu.VMEM((PAD, TOK), BF), pltpu.VMEM((ROWS - MROWS, PAD), BF)],
        flops=10**9,
        vmem=60,
    )(ids_t, prob_t, pmap, tok_t)
    got_x = lax.all_to_all(send_x, "dp", 0, 0, tiled=True)
    d_far_a, d_far_b = from_below(d_below[:368]), from_above(d_above[368:])
    wg = turn(wg_t, t)
    wu = turn(wu_t, t)
    x_a, x_b = got_x[: OWNERS // 2], got_x[OWNERS // 2 :]
    x_below_a, x_above_b = from_below(x_a), from_above(x_b)
    x_below_b, x_above_a = from_below(x_b), from_above(x_a)
    send_d = call(
        dispatch_d_body,
        struct((OWNERS, bd, 128)),
        in_specs=[sm()] + [vm()] * 6,
        out_specs=vm(),
        scratch_shapes=[pltpu.VMEM((3072, TOK), BF), pltpu.VMEM((ROWS - MROWS, FPAD), BF)],
        flops=2 * 10**9,
        vmem=60,
    )(t, pick, d_t, d_below, d_above, d_far_a, d_far_b)
    got_d = lax.all_to_all(send_d, "dp", 0, 0, tiled=True)
    x_far_a, x_far_b = from_below(x_below_a), from_above(x_above_b)
    act_spec = pl.BlockSpec((ROWS, 256), lambda i: (0, i))
    row_spec = pl.BlockSpec((256, FEAT), lambda i: (i, 0))
    mid = struct((ROWS, WID))
    half, half32 = struct((HALF, PAD)), struct((HALF, PAD), F32)
    act, fgu, x_rel = call(
        gate_up_body,
        (struct((ROWS, PAD)), struct((2, ROWS, PAD), F32), struct((SIDES, ROWS, PAD))),
        in_specs=[vm()] * 7 + [hbm()] * 2,
        out_specs=(hbm(),) * 3,
        scratch_shapes=[
            pltpu.VMEM((2, SIDES, WID, PAD), BF),
            pltpu.VMEM((ROWS, PAD), BF),
            pltpu.VMEM((2, ROWS, PAD), F32),
            pltpu.VMEM((SIDES, ROWS, PAD), BF),
            dma(6),
            dma(7),
        ],
        flops=5 * 10**9,
        vmem=GATE_VMEM,
    )(got_x, x_below_a, x_below_b, x_above_a, x_above_b, x_far_a, x_far_b, wg, wu)
    d_rows, gg, gu, prob, p_col, part_a, part_b = call(
        back_body,
        (struct((ROWS, FEAT)), mid, mid, struct((ROWS, 128), F32), struct((ROWS, 1), F32), half, half),
        in_specs=[hbm()] * 6,
        out_specs=(hbm(),) + (vm(),) * 6,
        scratch_shapes=[
            pltpu.VMEM((OWNERS, bd, 128), BF),
            pltpu.VMEM((WID, FEAT), BF),
            pltpu.VMEM((ROWS, PAD), BF),
            pltpu.VMEM((2, ROWS, PAD), F32),
            pltpu.VMEM((WID, PAD), BF),
            pltpu.VMEM((WID, PAD), BF),
            pltpu.VMEM((ROWS, FEAT), BF),
            dma(11),
            pltpu.SemaphoreType.DMA,
        ],
        flops=4 * 10**9,
        vmem=BACK_VMEM,
    )(got_d, wd, act, fgu, wg, wu)
    came_a, came_b = from_below(part_a), from_above(part_b)
    side = lambda k: pl.BlockSpec((1, WID, PAD), lambda i: (k, 0, 0))
    acts = [whole((ROWS, WID))] * 2
    tail = [whole((ROWS, 128))]
    send_a, send_b, keep_a, keep_b = call(
        near_dx_body,
        (half, half, half32, half32),
        grid=(1,),
        in_specs=acts + [side(1), side(1), side(3), side(3)] + tail,
        out_specs=(whole((HALF, PAD)),) * 4,
        flops=24 * 10**8,
        vmem=20,
    )(gg, gu, wg, wu, wg, wu, prob)
    below_b, above_a = from_below(send_a), from_above(send_b)
    own = call(
        own_dx_body,
        struct((ROWS, PAD), F32),
        grid=(1,),
        in_specs=acts + [side(0), side(0)] + tail,
        out_specs=whole((ROWS, PAD)),
        flops=12 * 10**8,
        vmem=20,
    )(gg, gu, wg, wu, prob)
    pass_a, pass_b = call(relay_body, (half, half), in_specs=[vm()] * 4, out_specs=(vm(), vm()), vmem=10)(
        keep_a, came_a, keep_b, came_b
    )
    below_a, above_b = from_below(pass_a), from_above(pass_b)
    gate_grad, up_grad = call(
        grad_pair_body,
        (struct((WID, FEAT)), struct((WID, FEAT))),
        grid=(3,),
        in_specs=[sm(), whole((SIDES, ROWS, PAD)), act_spec, act_spec],
        out_specs=(row_spec, row_spec),
        flops=5 * 10**9,
        vmem=20,
    )(t, x_rel, gg, gu)
    below_a, above_b, gate_grad, up_grad = hold(below_a, above_b, gate_grad, up_grad)
    send_back = call(
        sum_body,
        struct((OWNERS, bx, 128)),
        in_specs=[vm()] * 5,
        out_specs=vm(),
        scratch_shapes=[pltpu.VMEM((ROWS - MROWS, PAD), BF)],
        vmem=10,
    )(own, below_a, below_b, above_a, above_b)
    back = lax.all_to_all(send_back, "dp", 0, 0, tiled=True)
    down_grad = call(
        down_body,
        struct((WID, FEAT)),
        grid=(3,),
        in_specs=[whole((ROWS, FEAT)), act_spec, whole((ROWS, 1))],
        out_specs=row_spec,
        scratch_shapes=[pltpu.VMEM((ROWS, FEAT), BF)],
        flops=3 * 10**9,
        vmem=20,
    )(d_rows, act, p_col)
    dx_t, dp_t = call(
        combine_body,
        (struct((WID, TOK)), struct((TOP, TOK))),
        in_specs=[vm()] * 4,
        out_specs=(vm(), vm()),
        scratch_shapes=[pltpu.VMEM((ROWS, PAD), BF)],
        flops=10**9,
        vmem=10,
    )(back, pick, ids_t, pmap)
    return dx_t.T, gate_grad.T[None], up_grad.T[None], down_grad[None], dp_t.T


def solution(mesh):
    in_specs = (
        P("dp", "tensor"),
        P("dp", "tensor"),
        P("dp", None),
        P("dp", None),
        P(),
        P("dp", None, "tensor"),
        P("dp", None, "tensor"),
        P("dp", "tensor", None),
    )
    out_specs = (
        P("dp", "tensor"),
        P("dp", None, "tensor"),
        P("dp", None, "tensor"),
        P("dp", "tensor", None),
        P("dp", None),
    )

    return jax.shard_map(shards, mesh=mesh, in_specs=in_specs, out_specs=out_specs, check_vma=False)
```

profile of v0, /device:TPU:1, one launch (start us, length us, event | category | flops | bytes accessed | tf_op | source)
XLA Modules:
  0.0 163.9 jit_solution(16280644767655376366)
XLA Ops:
  0.6 2.1 %collective-permute-start = (bf16[720,384]{1,0:T(8,128)(2,1)}, bf16[720,384]{1,0:T(8,128)(2,1)S(1)}, u32[]{:S(2)}, u32[]{:S(2)}) collective-permute-start(bf16[720,384]{1,0:T(8,128)(2,1)} %bitcast.32), channel_id=1, source_target_pairs={{3,0},{0,1},{1,2},{2,3},{7,4},{4,5},{5,6},{6,7},{11,8},{8,9},{9,10... | collective-permute-start | bytes 1658888 | tf_op jit(solution)/shard_map/ppermute | solution.py:418
  2.7 1.4 collective-permute-start.1
  4.1 3.3 %shard_map.119 = (bf16[32,112,128]{2,1,0:T(8,128)(2,1)}, bf16[576,384]{1,0:T(8,128)(2,1)}) custom-call(s32[4,384]{1,0:T(4,128)} %bitcast.24, bf16[4,384]{1,0:T(4,128)(2,1)} %bitcast.35, s32[1,128]{1,0:T(1,128)} %bitcast.26, bf16[720,384]{1,0:T(8,128)(2,1)} %bitcast.31), custom_call_target="tpu_custom_call" | custom-call | flops 1000000000 | bytes 4194304 | tf_op jit(solution)/shard_map/pallas_call | solution.py:428
  7.4 9.4 %all-to-all-start.1 = ((bf16[32,112,128]{2,1,0:T(8,128)(2,1)}), bf16[32,112,128]{2,1,0:T(8,128)(2,1)S(1)}, u32[]{:S(2)}, u32[]{:S(2)}) async-start(bf16[32,112,128]{2,1,0:T(8,128)(2,1)} %get-tuple-element.36), calls=%async_computation.1 | async-start | bytes 1835008 | tf_op jit(solution)/shard_map/all_to_all | solution.py:437
  16.9 0.0 copy-start.15
  16.9 0.1 collective-permute-start.2
  17.0 0.0 copy-start.16
  17.1 2.7 %collective-permute-start.3 = (bf16[352,384]{1,0:T(8,128)(2,1)S(1)}, bf16[352,384]{1,0:T(8,128)(2,1)S(1)}, u32[]{:S(2)}, u32[]{:S(2)}) collective-permute-start(bf16[352,384]{1,0:T(8,128)(2,1)S(1)} %slice.17), channel_id=1, source_target_pairs={{1,0},{2,1},{3,2},{0,3},{5,4},{6,5},{7,6},{4,7},{9,8},{10,9},{11,1... | collective-permute-start | bytes 811016 | tf_op jit(solution)/shard_map/ppermute | solution.py:415
  19.8 4.7 %collective-permute-done.3.far_b_ref = bf16[352,384]{1,0:T(8,128)(2,1)S(1)} collective-permute-done((bf16[352,384]{1,0:T(8,128)(2,1)S(1)}, bf16[352,384]{1,0:T(8,128)(2,1)S(1)}, u32[]{:S(2)}, u32[]{:S(2)}) %collective-permute-start.3) | collective-permute-done | bytes 270368 | tf_op jit(solution)/shard_map/ppermute | solution.py:415
  24.5 1.2 collective-permute-done.2.far_a_ref
  25.7 0.7 copy-done.22
  26.4 5.7 %shard_map.120 = bf16[32,416,128]{2,1,0:T(8,128)(2,1)} custom-call(s32[1]{0:T(128)} %bitcast.t_ref, bf16[576,384]{1,0:T(8,128)(2,1)} %get-tuple-element.34.pick_ref, bf16[720,384]{1,0:T(8,128)(2,1)} %bitcast.34, bf16[720,384]{1,0:T(8,128)(2,1)} %copy-done.15, bf16[720,384]{1,0:T(8,128)(2,1)} %copy-done.16, bf16[368,384]{1,0:T(8,128)(2,1)} %copy-done.22, ...), custom_call_target="tpu_custom_call" | custom-call | flops 2000000000 | bytes 4194304 | tf_op jit(solution)/shard_map/pallas_call | solution.py:444
  32.1 0.4 all-to-all-done.1.refs_0_
  32.5 8.9 %all-to-all-start = ((bf16[32,416,128]{2,1,0:T(8,128)(2,1)}), bf16[32,416,128]{2,1,0:T(8,128)(2,1)}, u32[]{:S(2)}, u32[]{:S(2)}) async-start(bf16[32,416,128]{2,1,0:T(8,128)(2,1)} %shard_map.120), calls=%async_computation | async-start | bytes 6815744 | tf_op jit(solution)/shard_map/all_to_all | solution.py:453
  41.4 0.1 fusion
  41.5 2.7 %collective-permute-start.7 = (bf16[16,112,128]{2,1,0:T(8,128)(2,1)S(1)}, bf16[16,112,128]{2,1,0:T(8,128)(2,1)S(1)}, u32[]{:S(2)}, u32[]{:S(2)}) collective-permute-start(bf16[16,112,128]{2,1,0:T(8,128)(2,1)S(1)} %get-tuple-element.61), channel_id=1, source_target_pairs={{1,0},{2,1},{3,2},{0,3},{5,4},{6,5},{7,6},{4,7},{9,8},{10,9},{11,1... | collective-permute-start | bytes 1376264 | tf_op jit(solution)/shard_map/ppermute | solution.py:415
  44.2 2.7 %collective-permute-start.6 = (bf16[16,112,128]{2,1,0:T(8,128)(2,1)S(1)}, bf16[16,112,128]{2,1,0:T(8,128)(2,1)S(1)}, u32[]{:S(2)}, u32[]{:S(2)}) collective-permute-start(bf16[16,112,128]{2,1,0:T(8,128)(2,1)S(1)} %get-tuple-element.62), channel_id=1, source_target_pairs={{1,0},{2,1},{3,2},{0,3},{5,4},{6,5},{7,6},{4,7},{9,8},{10,9},{11,1... | collective-permute-start | bytes 1376264 | tf_op jit(solution)/shard_map/ppermute | solution.py:415
  46.9 6.9 %collective-permute-done.7.refs_4_ = bf16[16,112,128]{2,1,0:T(8,128)(2,1)S(1)} collective-permute-done((bf16[16,112,128]{2,1,0:T(8,128)(2,1)S(1)}, bf16[16,112,128]{2,1,0:T(8,128)(2,1)S(1)}, u32[]{:S(2)}, u32[]{:S(2)}) %collective-permute-start.7) | collective-permute-done | bytes 458784 | tf_op jit(solution)/shard_map/ppermute | solution.py:415
  53.8 3.5 %collective-permute-start.9 = (bf16[16,112,128]{2,1,0:T(8,128)(2,1)S(1)}, bf16[16,112,128]{2,1,0:T(8,128)(2,1)S(1)}, u32[]{:S(2)}, u32[]{:S(2)}) collective-permute-start(bf16[16,112,128]{2,1,0:T(8,128)(2,1)S(1)} %collective-permute-done.7.refs_4_), channel_id=1, source_target_pairs={{1,0},{2,1},{3,2},{0,3},{5,4},{6,5},{7,6},{4,7},{9,8},{10,9},{11,1... | collective-permute-start | bytes 1376264 | tf_op jit(solution)/shard_map/ppermute | solution.py:415
  57.3 6.7 %shard_map.122.refs_8_.wu_hbm.wu_ref.wua_ref.wub_ref = bf16[4,720,768]{2,1,0:T(8,128)(2,1)} custom-call(s32[1]{0:T(128)} %bitcast.t_ref, bf16[720,2880]{1,0:T(8,128)(2,1)} %bitcast.28), custom_call_target="tpu_custom_call" | custom-call | bytes 4194304 | tf_op jit(solution)/shard_map/pallas_call | solution.py:384
  64.0 6.5 %shard_map.121.refs_7_.wg_hbm.wg_ref.wga_ref.wgb_ref = bf16[4,720,768]{2,1,0:T(8,128)(2,1)} custom-call(s32[1]{0:T(128)} %bitcast.t_ref, bf16[720,2880]{1,0:T(8,128)(2,1)} %bitcast.29), custom_call_target="tpu_custom_call" | custom-call | bytes 4194304 | tf_op jit(solution)/shard_map/pallas_call | solution.py:384
  70.6 2.8 %collective-permute-done.9.refs_6_ = bf16[16,112,128]{2,1,0:T(8,128)(2,1)S(1)} collective-permute-done((bf16[16,112,128]{2,1,0:T(8,128)(2,1)S(1)}, bf16[16,112,128]{2,1,0:T(8,128)(2,1)S(1)}, u32[]{:S(2)}, u32[]{:S(2)}) %collective-permute-start.9) | collective-permute-done | bytes 458784 | tf_op jit(solution)/shard_map/ppermute | solution.py:415
  73.4 3.2 %collective-permute-done.8.refs_5_ = bf16[16,112,128]{2,1,0:T(8,128)(2,1)} collective-permute-done((bf16[16,112,128]{2,1,0:T(8,128)(2,1)S(1)}, bf16[16,112,128]{2,1,0:T(8,128)(2,1)}, u32[]{:S(2)}, u32[]{:S(2)}) %collective-permute-start.8) | collective-permute-done | bytes 458784 | tf_op jit(solution)/shard_map/ppermute | solution.py:418
  76.7 12.1 %shard_map.123 = (bf16[576,768]{1,0:T(8,128)(2,1)}, f32[2,576,768]{2,1,0:T(8,128)}, bf16[4,576,768]{2,1,0:T(8,128)(2,1)}) custom-call(bf16[32,112,128]{2,1,0:T(8,128)(2,1)} %copy-done.14, bf16[16,112,128]{2,1,0:T(8,128)(2,1)} %copy-done.18, bf16[16,112,128]{2,1,0:T(8,128)(2,1)} %copy-done.19, bf16[16,112,128]{2,1,0:T(8,128)(2,1)} %copy-done.20, ...), custom_call_target="tpu_custom_call" | custom-call | flops 5000000000 | bytes 4194304 | tf_op jit(solution)/shard_map/pallas_call | solution.py:459
  88.8 14.6 %shard_map.124 = (bf16[576,2880]{1,0:T(8,128)(2,1)}, bf16[576,720]{1,0:T(8,128)(2,1)}, bf16[576,720]{1,0:T(8,128)(2,1)}, f32[576,128]{1,0:T(8,128)}, f32[576,1]{...) custom-call(bf16[32,416,128]{2,1,0:T(8,128)(2,1)} %all-to-all-done.got_hbm, bf16[720,2880]{1,0:T(8,128)(2,1)} %bitcast.30, ...), custom_call_target="tpu_custom_call" | custom-call | flops 4000000000 | bytes 4194304 | tf_op jit(solution)/shard_map/pallas_call | solution.py:475
  103.4 0.3 collective-permute-start.10
  103.7 2.7 %collective-permute-start.11 = (bf16[288,768]{1,0:T(8,128)(2,1)}, bf16[288,768]{1,0:T(8,128)(2,1)S(1)}, u32[]{:S(2)}, u32[]{:S(2)}) collective-permute-start(bf16[288,768]{1,0:T(8,128)(2,1)} %get-tuple-element.45), channel_id=1, source_target_pairs={{1,0},{2,1},{3,2},{0,3},{5,4},{6,5},{7,6},{4,7},{9,8},{10,9},{11,1... | collective-permute-start | bytes 1327112 | tf_op jit(solution)/shard_map/ppermute | solution.py:415
  106.4 2.3 %copy-done = bf16[4,720,768]{2,1,0:T(8,128)(2,1)S(1)} copy-done((bf16[4,720,768]{2,1,0:T(8,128)(2,1)S(1)}, bf16[4,720,768]{2,1,0:T(8,128)(2,1)}, u32[]{:S(2)}) %copy-start) | copy-done | bytes 4423704
  108.7 1.2 copy-done.1
  109.8 1.2 copy-done.3
  111.0 1.0 copy-done.5
  112.0 2.9 %shard_map.126 = (bf16[288,768]{1,0:T(8,128)(2,1)S(1)}, bf16[288,768]{1,0:T(8,128)(2,1)S(1)}, f32[288,768]{1,0:T(8,128)S(1)}, f32[288,768]{1,0:T(8,128)S(1)}) custom-call(bf16[576,720]{1,0:T(8,128)(2,1)S(1)} %copy-done.1, bf16[576,720]{1,0:T(8,128)(2,1)S(1)} %copy-done.3, bf16[4,720,768]{2,1,0:T(8,128)(2,1)S(1)} %copy-done, ...), custom_call_target="tpu_custom_call" | custom-call | flops 2400000000 | bytes 4194304 | tf_op jit(solution)/shard_map/pallas_call | solution.py:498
  114.9 0.1 collective-permute-start.14
  115.0 0.0 copy-start.2
  115.0 0.0 copy-start.13
  115.0 2.6 %collective-permute-start.15 = (bf16[288,768]{1,0:T(8,128)(2,1)S(1)}, bf16[288,768]{1,0:T(8,128)(2,1)S(1)}, u32[]{:S(2)}, u32[]{:S(2)}) collective-permute-start(bf16[288,768]{1,0:T(8,128)(2,1)S(1)} %get-tuple-element.53), channel_id=1, source_target_pairs={{1,0},{2,1},{3,2},{0,3},{5,4},{6,5},{7,6},{4,7},{9,8},{10,9},{11,1... | collective-permute-start | bytes 1327112 | tf_op jit(solution)/shard_map/ppermute | solution.py:415
  117.6 1.5 shard_map.125.own_ref
  119.2 0.5 shard_map.127
  119.7 0.1 collective-permute-start.12
  119.8 2.7 %collective-permute-start.13 = (bf16[288,768]{1,0:T(8,128)(2,1)S(1)}, bf16[288,768]{1,0:T(8,128)(2,1)S(1)}, u32[]{:S(2)}, u32[]{:S(2)}) collective-permute-start(bf16[288,768]{1,0:T(8,128)(2,1)S(1)} %get-tuple-element.47), channel_id=1, source_target_pairs={{1,0},{2,1},{3,2},{0,3},{5,4},{6,5},{7,6},{4,7},{9,8},{10,9},{11,1... | collective-permute-start | bytes 1327112 | tf_op jit(solution)/shard_map/ppermute | solution.py:415
  122.5 9.7 %shard_map.128 = (bf16[720,2880]{1,0:T(8,128)(2,1)}, bf16[720,2880]{1,0:T(8,128)(2,1)}) custom-call(s32[1]{0:T(128)} %bitcast.t_ref, bf16[4,576,768]{2,1,0:T(8,128)(2,1)S(1)} %copy-done.13, bf16[576,720]{1,0:T(8,128)(2,1)S(1)} %copy-done.2, bf16[576,720]{1,0:T(8,128)(2,1)S(1)} %copy-done.4), custom_call_target="tpu_custom_call" | custom-call | flops 5000000000 | bytes 4194304 | tf_op jit(solution)/shard_map/pallas_call | solution.py:521
  132.2 3.1 %collective-permute-done.12.below_a = bf16[288,768]{1,0:T(8,128)(2,1)S(1)} collective-permute-done((bf16[288,768]{1,0:T(8,128)(2,1)S(1)}, bf16[288,768]{1,0:T(8,128)(2,1)S(1)}, u32[]{:S(2)}, u32[]{:S(2)}) %collective-permute-start.12) | collective-permute-done | bytes 442400 | tf_op jit(solution)/shard_map/ppermute | solution.py:418
  135.4 1.4 shard_map.129
  136.8 9.8 %all-to-all-start.2 = ((bf16[32,112,128]{2,1,0:T(8,128)(2,1)}), bf16[32,112,128]{2,1,0:T(8,128)(2,1)S(1)}, u32[]{:S(2)}, u32[]{:S(2)}) async-start(bf16[32,112,128]{2,1,0:T(8,128)(2,1)} %shard_map.129), calls=%async_computation.2 | async-start | bytes 1835008 | tf_op jit(solution)/shard_map/all_to_all | solution.py:539
  146.6 2.0 %copy-done.8 = bf16[576,2880]{1,0:T(8,128)(2,1)S(1)} copy-done((bf16[576,2880]{1,0:T(8,128)(2,1)S(1)}, bf16[576,2880]{1,0:T(8,128)(2,1)}, u32[]{:S(2)}) %copy-start.8) | copy-done | bytes 3317784
  148.5 6.0 %shard_map.131 = bf16[720,2880]{1,0:T(8,128)(2,1)} custom-call(bf16[576,2880]{1,0:T(8,128)(2,1)S(1)} %copy-done.8, bf16[576,768]{1,0:T(8,128)(2,1)S(1)} %copy-done.7, f32[576,1]{1,0:T(8,128)S(1)} %copy-done.9), custom_call_target="tpu_custom_call" | custom-call | flops 3000000000 | bytes 4194304 | tf_op jit(solution)/shard_map/pallas_call | solution.py:540
  154.5 7.7 %all-to-all-done.2.back_ref = bf16[32,112,128]{2,1,0:T(8,128)(2,1)S(1)} async-done(((bf16[32,112,128]{2,1,0:T(8,128)(2,1)}), bf16[32,112,128]{2,1,0:T(8,128)(2,1)S(1)}, u32[]{:S(2)}, u32[]{:S(2)}) %all-to-all-start.2) | async-done | bytes 917536 | tf_op jit(solution)/shard_map/all_to_all | solution.py:539
  162.2 1.7 %shard_map.130 = (bf16[720,384]{1,0:T(8,128)(2,1)}, bf16[4,384]{1,0:T(4,128)(2,1)}) custom-call(bf16[32,112,128]{2,1,0:T(8,128)(2,1)S(1)} %all-to-all-done.2.back_ref, bf16[576,384]{1,0:T(8,128)(2,1)S(1)} %copy-done.12, s32[4,384]{1,0:T(4,128)S(1)} %bitcast.25, s32[1,128]{1,0:T(1,128)S(1)} %bitcast.27), custom_call_target="tpu_custom_call" | custom-call | flops 1000000000 | bytes 4194304 | tf_op jit(solution)/shard_map/pallas_call | solution.py:550
  (59 shorter events, 0.2 us)
Async XLA Ops:
  0.6 16.2 %collective-permute-start = (bf16[720,384]{1,0:T(8,128)(2,1)}, bf16[720,384]{1,0:T(8,128)(2,1)S(1)}, u32[]{:S(2)}, u32[]{:S(2)}) collective-permute-start(bf16[720,384]{1,0:T(8,128)(2,1)} %bitcast.32), channel_id=1, source_target_pairs={{3,0},{0,1},{1,2},{2,3},{7,4},{4,5},{5,6},{6,7},{11,8},{8,9},{9,10... | collective-permute-start | bytes 1658888 | tf_op jit(solution)/shard_map/ppermute | solution.py:418
  2.7 14.3 %collective-permute-start.1 = (bf16[720,384]{1,0:T(8,128)(2,1)}, bf16[720,384]{1,0:T(8,128)(2,1)S(1)}, u32[]{:S(2)}, u32[]{:S(2)}) collective-permute-start(bf16[720,384]{1,0:T(8,128)(2,1)} %bitcast.33), channel_id=1, source_target_pairs={{1,0},{2,1},{3,2},{0,3},{5,4},{6,5},{7,6},{4,7},{9,8},{10,9},{11,1... | collective-permute-start | bytes 1658888 | tf_op jit(solution)/shard_map/ppermute | solution.py:415
  7.4 25.1 %all-to-all-start.1 = ((bf16[32,112,128]{2,1,0:T(8,128)(2,1)}), bf16[32,112,128]{2,1,0:T(8,128)(2,1)S(1)}, u32[]{:S(2)}, u32[]{:S(2)}) async-start(bf16[32,112,128]{2,1,0:T(8,128)(2,1)} %get-tuple-element.36), calls=%async_computation.1 | async-start | bytes 1835008 | tf_op jit(solution)/shard_map/all_to_all | solution.py:437
  16.9 8.8 %copy-start.15 = (bf16[720,384]{1,0:T(8,128)(2,1)}, bf16[720,384]{1,0:T(8,128)(2,1)S(1)}, u32[]{:S(2)}) copy-start(bf16[720,384]{1,0:T(8,128)(2,1)S(1)} %collective-permute-done.below_ref) | copy-start | bytes 1658884
  16.9 8.8 %collective-permute-start.2 = (bf16[368,384]{1,0:T(8,128)(2,1)S(1)}, bf16[368,384]{1,0:T(8,128)(2,1)S(1)}, u32[]{:S(2)}, u32[]{:S(2)}) collective-permute-start(bf16[368,384]{1,0:T(8,128)(2,1)S(1)} %slice.16), channel_id=1, source_target_pairs={{3,0},{0,1},{1,2},{2,3},{7,4},{4,5},{5,6},{6,7},{11,8},{8,9},{9,10... | collective-permute-start | bytes 847880 | tf_op jit(solution)/shard_map/ppermute | solution.py:418
  17.0 8.7 %copy-start.16 = (bf16[720,384]{1,0:T(8,128)(2,1)}, bf16[720,384]{1,0:T(8,128)(2,1)S(1)}, u32[]{:S(2)}) copy-start(bf16[720,384]{1,0:T(8,128)(2,1)S(1)} %collective-permute-done.1.above_ref) | copy-start | bytes 1658884
  17.1 7.4 %collective-permute-start.3 = (bf16[352,384]{1,0:T(8,128)(2,1)S(1)}, bf16[352,384]{1,0:T(8,128)(2,1)S(1)}, u32[]{:S(2)}, u32[]{:S(2)}) collective-permute-start(bf16[352,384]{1,0:T(8,128)(2,1)S(1)} %slice.17), channel_id=1, source_target_pairs={{1,0},{2,1},{3,2},{0,3},{5,4},{6,5},{7,6},{4,7},{9,8},{10,9},{11,1... | collective-permute-start | bytes 811016 | tf_op jit(solution)/shard_map/ppermute | solution.py:415
  24.5 1.2 copy-start.23
  25.7 0.7 copy-start.22
  32.5 9.0 %copy-start.14 = (bf16[32,112,128]{2,1,0:T(8,128)(2,1)}, bf16[32,112,128]{2,1,0:T(8,128)(2,1)S(1)}, u32[]{:S(2)}) copy-start(bf16[32,112,128]{2,1,0:T(8,128)(2,1)S(1)} %all-to-all-done.1.refs_0_) | copy-start | bytes 2752516
  32.5 56.3 %all-to-all-start = ((bf16[32,416,128]{2,1,0:T(8,128)(2,1)}), bf16[32,416,128]{2,1,0:T(8,128)(2,1)}, u32[]{:S(2)}, u32[]{:S(2)}) async-start(bf16[32,416,128]{2,1,0:T(8,128)(2,1)} %shard_map.120), calls=%async_computation | async-start | bytes 6815744 | tf_op jit(solution)/shard_map/all_to_all | solution.py:453
  41.5 12.3 %collective-permute-start.7 = (bf16[16,112,128]{2,1,0:T(8,128)(2,1)S(1)}, bf16[16,112,128]{2,1,0:T(8,128)(2,1)S(1)}, u32[]{:S(2)}, u32[]{:S(2)}) collective-permute-start(bf16[16,112,128]{2,1,0:T(8,128)(2,1)S(1)} %get-tuple-element.61), channel_id=1, source_target_pairs={{1,0},{2,1},{3,2},{0,3},{5,4},{6,5},{7,6},{4,7},{9,8},{10,9},{11,1... | collective-permute-start | bytes 1376264 | tf_op jit(solution)/shard_map/ppermute | solution.py:415
  44.2 13.1 %collective-permute-start.4 = (bf16[16,112,128]{2,1,0:T(8,128)(2,1)S(1)}, bf16[16,112,128]{2,1,0:T(8,128)(2,1)S(1)}, u32[]{:S(2)}, u32[]{:S(2)}) collective-permute-start(bf16[16,112,128]{2,1,0:T(8,128)(2,1)S(1)} %get-tuple-element.62), channel_id=1, source_target_pairs={{3,0},{0,1},{1,2},{2,3},{7,4},{4,5},{5,6},{6,7},{11,8},{8,9},{9,10... | collective-permute-start | bytes 1376264 | tf_op jit(solution)/shard_map/ppermute | solution.py:418
  44.2 26.4 %collective-permute-start.5 = (bf16[16,112,128]{2,1,0:T(8,128)(2,1)S(1)}, bf16[16,112,128]{2,1,0:T(8,128)(2,1)S(1)}, u32[]{:S(2)}, u32[]{:S(2)}) collective-permute-start(bf16[16,112,128]{2,1,0:T(8,128)(2,1)S(1)} %get-tuple-element.61), channel_id=1, source_target_pairs={{3,0},{0,1},{1,2},{2,3},{7,4},{4,5},{5,6},{6,7},{11,8},{8,9},{9,10... | collective-permute-start | bytes 1376264 | tf_op jit(solution)/shard_map/ppermute | solution.py:418
  44.2 26.4 %collective-permute-start.6 = (bf16[16,112,128]{2,1,0:T(8,128)(2,1)S(1)}, bf16[16,112,128]{2,1,0:T(8,128)(2,1)S(1)}, u32[]{:S(2)}, u32[]{:S(2)}) collective-permute-start(bf16[16,112,128]{2,1,0:T(8,128)(2,1)S(1)} %get-tuple-element.62), channel_id=1, source_target_pairs={{1,0},{2,1},{3,2},{0,3},{5,4},{6,5},{7,6},{4,7},{9,8},{10,9},{11,1... | collective-permute-start | bytes 1376264 | tf_op jit(solution)/shard_map/ppermute | solution.py:415
  53.8 10.2 %copy-start.17 = (bf16[16,112,128]{2,1,0:T(8,128)(2,1)}, bf16[16,112,128]{2,1,0:T(8,128)(2,1)S(1)}, u32[]{:S(2)}) copy-start(bf16[16,112,128]{2,1,0:T(8,128)(2,1)S(1)} %collective-permute-done.7.refs_4_) | copy-start | bytes 1376260
  53.8 19.7 %collective-permute-start.9 = (bf16[16,112,128]{2,1,0:T(8,128)(2,1)S(1)}, bf16[16,112,128]{2,1,0:T(8,128)(2,1)S(1)}, u32[]{:S(2)}, u32[]{:S(2)}) collective-permute-start(bf16[16,112,128]{2,1,0:T(8,128)(2,1)S(1)} %collective-permute-done.7.refs_4_), channel_id=1, source_target_pairs={{1,0},{2,1},{3,2},{0,3},{5,4},{6,5},{7,6},{4,7},{9,8},{10,9},{11,1... | collective-permute-start | bytes 1376264 | tf_op jit(solution)/shard_map/ppermute | solution.py:415
  57.3 6.7 %copy-start.18 = (bf16[16,112,128]{2,1,0:T(8,128)(2,1)}, bf16[16,112,128]{2,1,0:T(8,128)(2,1)S(1)}, u32[]{:S(2)}) copy-start(bf16[16,112,128]{2,1,0:T(8,128)(2,1)S(1)} %collective-permute-done.4.refs_1_) | copy-start | bytes 1376260
  57.3 19.4 %collective-permute-start.8 = (bf16[16,112,128]{2,1,0:T(8,128)(2,1)S(1)}, bf16[16,112,128]{2,1,0:T(8,128)(2,1)}, u32[]{:S(2)}, u32[]{:S(2)}) collective-permute-start(bf16[16,112,128]{2,1,0:T(8,128)(2,1)S(1)} %collective-permute-done.4.refs_1_), channel_id=1, source_target_pairs={{3,0},{0,1},{1,2},{2,3},{7,4},{4,5},{5,6},{6,7},{11,8},{8,9},{9,10... | collective-permute-start | bytes 1376264 | tf_op jit(solution)/shard_map/ppermute | solution.py:418
  70.6 6.1 %copy-start.19 = (bf16[16,112,128]{2,1,0:T(8,128)(2,1)}, bf16[16,112,128]{2,1,0:T(8,128)(2,1)S(1)}, u32[]{:S(2)}) copy-start(bf16[16,112,128]{2,1,0:T(8,128)(2,1)S(1)} %collective-permute-done.5.refs_2_) | copy-start | bytes 1376260
  70.6 6.1 %copy-start.20 = (bf16[16,112,128]{2,1,0:T(8,128)(2,1)}, bf16[16,112,128]{2,1,0:T(8,128)(2,1)S(1)}, u32[]{:S(2)}) copy-start(bf16[16,112,128]{2,1,0:T(8,128)(2,1)S(1)} %collective-permute-done.6.refs_3_) | copy-start | bytes 1376260
  73.4 3.2 %copy-start.21 = (bf16[16,112,128]{2,1,0:T(8,128)(2,1)}, bf16[16,112,128]{2,1,0:T(8,128)(2,1)S(1)}, u32[]{:S(2)}) copy-start(bf16[16,112,128]{2,1,0:T(8,128)(2,1)S(1)} %collective-permute-done.9.refs_6_) | copy-start | bytes 1376260
  76.7 29.7 %slice-start = ((s8[4423680]{0:T(1024)(128)(4,1)}), s8[229376]{0:T(1024)(128)(4,1)S(1)}, s32[]{:S(2)}) async-start(s8[4423680]{0:T(1024)(128)(4,1)} %bitcast.22), calls=%async_computation.3 | async-start | bytes 458752
  88.8 17.6 %slice-start.1 = ((s8[4423680]{0:T(1024)(128)(4,1)}), s8[4194304]{0:T(1024)(128)(4,1)S(1)}, s32[]{:S(2)}) async-start(s8[4423680]{0:T(1024)(128)(4,1)} %bitcast.22), calls=%async_computation.4 | async-start | bytes 8388608
  103.4 15.8 %collective-permute-start.10 = (bf16[288,768]{1,0:T(8,128)(2,1)}, bf16[288,768]{1,0:T(8,128)(2,1)S(1)}, u32[]{:S(2)}, u32[]{:S(2)}) collective-permute-start(bf16[288,768]{1,0:T(8,128)(2,1)} %get-tuple-element.43), channel_id=1, source_target_pairs={{3,0},{0,1},{1,2},{2,3},{7,4},{4,5},{5,6},{6,7},{11,8},{8,9},{9,10... | collective-permute-start | bytes 1327112 | tf_op jit(solution)/shard_map/ppermute | solution.py:418
  103.7 15.5 %collective-permute-start.11 = (bf16[288,768]{1,0:T(8,128)(2,1)}, bf16[288,768]{1,0:T(8,128)(2,1)S(1)}, u32[]{:S(2)}, u32[]{:S(2)}) collective-permute-start(bf16[288,768]{1,0:T(8,128)(2,1)} %get-tuple-element.45), channel_id=1, source_target_pairs={{1,0},{2,1},{3,2},{0,3},{5,4},{6,5},{7,6},{4,7},{9,8},{10,9},{11,1... | collective-permute-start | bytes 1327112 | tf_op jit(solution)/shard_map/ppermute | solution.py:415
  106.4 2.3 %copy-start = (bf16[4,720,768]{2,1,0:T(8,128)(2,1)S(1)}, bf16[4,720,768]{2,1,0:T(8,128)(2,1)}, u32[]{:S(2)}) copy-start(bf16[4,720,768]{2,1,0:T(8,128)(2,1)} %shard_map.121.refs_7_.wg_hbm.wg_ref.wga_ref.wgb_ref) | copy-start | bytes 13271044
  108.7 1.2 copy-start.1
  109.8 1.2 copy-start.3
  111.0 1.0 copy-start.5
  112.0 5.7 %copy-start.4 = (bf16[576,720]{1,0:T(8,128)(2,1)S(1)}, bf16[576,720]{1,0:T(8,128)(2,1)}, u32[]{:S(2)}) copy-start(bf16[576,720]{1,0:T(8,128)(2,1)} %get-tuple-element.40.gu_ref) | copy-start | bytes 2488324
  112.0 5.7 %copy-start.6 = (f32[576,128]{1,0:T(8,128)S(1)}, f32[576,128]{1,0:T(8,128)}, u32[]{:S(2)}) copy-start(f32[576,128]{1,0:T(8,128)} %get-tuple-element.41.prob_ref) | copy-start | bytes 884740
  114.9 20.5 %collective-permute-start.14 = (bf16[288,768]{1,0:T(8,128)(2,1)S(1)}, bf16[288,768]{1,0:T(8,128)(2,1)S(1)}, u32[]{:S(2)}, u32[]{:S(2)}) collective-permute-start(bf16[288,768]{1,0:T(8,128)(2,1)S(1)} %get-tuple-element.52), channel_id=1, source_target_pairs={{3,0},{0,1},{1,2},{2,3},{7,4},{4,5},{5,6},{6,7},{11,8},{8,9},{9,10... | collective-permute-start | bytes 1327112 | tf_op jit(solution)/shard_map/ppermute | solution.py:418
  115.0 7.5 %copy-start.2 = (bf16[576,720]{1,0:T(8,128)(2,1)S(1)}, bf16[576,720]{1,0:T(8,128)(2,1)}, u32[]{:S(2)}) copy-start(bf16[576,720]{1,0:T(8,128)(2,1)} %get-tuple-element.39.gg_ref) | copy-start | bytes 2488324
  115.0 7.5 %copy-start.13 = (bf16[4,576,768]{2,1,0:T(8,128)(2,1)S(1)}, bf16[4,576,768]{2,1,0:T(8,128)(2,1)}, u32[]{:S(2)}) copy-start(bf16[4,576,768]{2,1,0:T(8,128)(2,1)} %get-tuple-element.48.x_ref) | copy-start | bytes 10616836
  115.0 20.4 %collective-permute-start.15 = (bf16[288,768]{1,0:T(8,128)(2,1)S(1)}, bf16[288,768]{1,0:T(8,128)(2,1)S(1)}, u32[]{:S(2)}, u32[]{:S(2)}) collective-permute-start(bf16[288,768]{1,0:T(8,128)(2,1)S(1)} %get-tuple-element.53), channel_id=1, source_target_pairs={{1,0},{2,1},{3,2},{0,3},{5,4},{6,5},{7,6},{4,7},{9,8},{10,9},{11,1... | collective-permute-start | bytes 1327112 | tf_op jit(solution)/shard_map/ppermute | solution.py:415
  119.7 15.6 %collective-permute-start.12 = (bf16[288,768]{1,0:T(8,128)(2,1)S(1)}, bf16[288,768]{1,0:T(8,128)(2,1)S(1)}, u32[]{:S(2)}, u32[]{:S(2)}) collective-permute-start(bf16[288,768]{1,0:T(8,128)(2,1)S(1)} %get-tuple-element.46), channel_id=1, source_target_pairs={{3,0},{0,1},{1,2},{2,3},{7,4},{4,5},{5,6},{6,7},{11,8},{8,9},{9,10... | collective-permute-start | bytes 1327112 | tf_op jit(solution)/shard_map/ppermute | solution.py:418
  119.8 15.6 %collective-permute-start.13 = (bf16[288,768]{1,0:T(8,128)(2,1)S(1)}, bf16[288,768]{1,0:T(8,128)(2,1)S(1)}, u32[]{:S(2)}, u32[]{:S(2)}) collective-permute-start(bf16[288,768]{1,0:T(8,128)(2,1)S(1)} %get-tuple-element.47), channel_id=1, source_target_pairs={{1,0},{2,1},{3,2},{0,3},{5,4},{6,5},{7,6},{4,7},{9,8},{10,9},{11,1... | collective-permute-start | bytes 1327112 | tf_op jit(solution)/shard_map/ppermute | solution.py:415
  132.2 14.3 %copy-start.7 = (bf16[576,768]{1,0:T(8,128)(2,1)S(1)}, bf16[576,768]{1,0:T(8,128)(2,1)}, u32[]{:S(2)}) copy-start(bf16[576,768]{1,0:T(8,128)(2,1)} %get-tuple-element.37.act_hbm.act_ref) | copy-start | bytes 2654212
  132.2 14.3 %copy-start.9 = (f32[576,1]{1,0:T(8,128)S(1)}, f32[576,1]{1,0:T(8,128)}, u32[]{:S(2)}) copy-start(f32[576,1]{1,0:T(8,128)} %get-tuple-element.59.p_ref) | copy-start | bytes 6916
  136.8 25.4 %all-to-all-start.2 = ((bf16[32,112,128]{2,1,0:T(8,128)(2,1)}), bf16[32,112,128]{2,1,0:T(8,128)(2,1)S(1)}, u32[]{:S(2)}, u32[]{:S(2)}) async-start(bf16[32,112,128]{2,1,0:T(8,128)(2,1)} %shard_map.129), calls=%async_computation.2 | async-start | bytes 1835008 | tf_op jit(solution)/shard_map/all_to_all | solution.py:539
  146.6 2.0 %copy-start.8 = (bf16[576,2880]{1,0:T(8,128)(2,1)S(1)}, bf16[576,2880]{1,0:T(8,128)(2,1)}, u32[]{:S(2)}) copy-start(bf16[576,2880]{1,0:T(8,128)(2,1)} %get-tuple-element.58.d_ref) | copy-start | bytes 9953284
  148.5 13.7 %copy-start.10 = (s32[384,4]{0,1:T(4,128)S(1)}, s32[384,4]{0,1:T(4,128)}, u32[]{:S(2)}) copy-start(s32[384,4]{0,1:T(4,128)} %param.11) | copy-start | bytes 18436
  148.5 13.7 %copy-start.11 = (s32[128]{0:T(128)S(1)}, s32[128]{0:T(128)}, u32[]{:S(2)}) copy-start(s32[128]{0:T(128)} %param.12) | copy-start | bytes 1540
  148.5 13.7 %copy-start.12 = (bf16[576,384]{1,0:T(8,128)(2,1)S(1)}, bf16[576,384]{1,0:T(8,128)(2,1)}, u32[]{:S(2)}) copy-start(bf16[576,384]{1,0:T(8,128)(2,1)} %get-tuple-element.34.pick_ref) | copy-start | bytes 1327108
where the time goes:
time: 165 us; the launch traced here: 164 us
  Pallas kernels  72.8 us (44%)
  starting transfers between devices  51.7 us (31%)
  waiting for transfers between devices  30.1 us (18%)
  local copies, waits for them, and re-layouts  8.4 us (5%)
    ppermute x8, starting transfers between devices, from_above(): return lax.ppermute(value, 'tensor', above)  20.9 us
    pallas_call x1, Pallas kernels, shards(): call(back_body, (struct((ROWS, FEAT)), mid, mid, struct((ROWS, 128), F32)...  14.6 us
    ppermute x8, waiting for transfers between devices, from_above(): return lax.ppermute(value, 'tensor', above)  14.5 us
    pallas_call x2, Pallas kernels, turn(): call(turn_body, struct((SIDES, WID, PAD)), grid=(3,), in_specs=[sm(), pl....  13.3 us
    pallas_call x1, Pallas kernels, shards(): call(gate_up_body, (struct((ROWS, PAD)), struct((2, ROWS, PAD), F32), str...  12.1 us
    all_to_all x1, starting transfers between devices, shards(): back = lax.all_to_all(send_back, 'dp', 0, 0, tiled=True)  9.76 us
    pallas_call x1, Pallas kernels, shards(): call(grad_pair_body, (struct((WID, FEAT)), struct((WID, FEAT))), grid=(3,...  9.75 us
    all_to_all x1, starting transfers between devices, shards(): got_x = lax.all_to_all(send_x, 'dp', 0, 0, tiled=True)  9.44 us
  transfers between devices with their start and end apart: 19, of which 8 were waited for; matrix products, arithmetic and copies ran while one was open for 0% of the time, Pallas kernels for 34%

commit v1 on v0

--- a/solution.py
+++ b/solution.py
@@ -21,7 +21,10 @@
 FPAD = 2944
 SIDES = 4
 GATE_VMEM = 58
-BACK_VMEM = 55
+TURN_VMEM = 59
+NEAR_VMEM = 20
+SEND_VMEM = 44
+BACK_VMEM = 52
 PROB = 720
 
 BF = jnp.bfloat16
@@ -200,10 +203,13 @@
 
 
 def gate_up_body(*refs):
-    x_refs, w_refs, (act_out, mid_out, x_out), (w, act, mid, x, in_sems, out_sems) = refs[:7], refs[7:9], refs[9:12], refs[12:]
-    loads = copies(
-        [(w_refs[n].at[:, lo : lo + size, :], w.at[n, :, lo : lo + size, :]) for lo, size in CHUNKS for n in range(2)], in_sems
-    )
+    x_refs, w_refs, (act_out, mid_out, x_out), (got, w, act, mid, x, got_sems, in_sems, out_sems) = refs[:7], refs[7:9], refs[9:12], refs[12:]
+    peers = [slice(0, OWNERS)] + [slice(0, OWNERS // 2), slice(OWNERS // 2, OWNERS)] * 3
+    sides = [0, 3, 3, 1, 1, 2, 2]
+    blocks = [got.at[side, part] for side, part in zip(sides, peers)]
+    got_loads = copies(list(zip(x_refs, blocks)), got_sems)
+    pairs = [(w_refs[n].at[:, lo : lo + size, :], w.at[n, :, lo : lo + size, :]) for lo, size in CHUNKS for n in range(2)]
+    loads = copies(pairs[:2], in_sems)
 
     def keep(side):
         def store(row, lane, value):
@@ -211,10 +217,10 @@
 
         return store
 
-    unpack(x_refs[0], PAD, keep(0))
-    for n, side in enumerate((3, 1, 2)):
-        unpack(x_refs[2 * n + 1], PAD, keep(side), 0)
-        unpack(x_refs[2 * n + 2], PAD, keep(side), OWNERS // 2)
+    for n, (side, part) in enumerate(zip(sides, peers)):
+        got_loads[n].wait()
+        unpack(blocks[n], PAD, keep(side), part.start)
+    loads += copies(pairs[2:], in_sems.at[2:])
     stores = [pltpu.make_async_copy(x, x_out, out_sems.at[6])]
     stores[0].start()
     for c, (lo, size) in enumerate(CHUNKS):
@@ -225,14 +231,13 @@
         sig = 1.0 / (1.0 + jnp.exp(-SWISH_SLOPE * gate))
         glu = gate * sig
         act[:, lo : lo + size] = (glu * up1).astype(BF)
-        mid[0, :, lo : lo + size] = up1 * (sig + SWISH_SLOPE * glu * (1.0 - sig))
-        mid[1, :, lo : lo + size] = glu
+        mid[0, :, lo : lo + size] = (up1 * (sig + SWISH_SLOPE * glu * (1.0 - sig))).astype(BF)
+        mid[1, :, lo : lo + size] = glu.astype(BF)
         if c == 2:
             tile = x[0, :, 640:768].astype(F32)
             p_col = jnp.sum(jnp.where(iota((ROWS, 128), 1) == PROB - 640, tile, 0.0), axis=1, keepdims=True)
-            mid[0, :, WID:PAD] = jnp.broadcast_to(p_col, (ROWS, PAD - WID))
-            mid[1, :, WID:PAD] = jnp.zeros((ROWS, PAD - WID), F32)
-            act[:, WID:PAD] = jnp.zeros((ROWS, PAD - WID), BF)
+            act[:, WID:PAD] = jnp.broadcast_to(p_col, (ROWS, PAD - WID)).astype(BF)
+            mid[:, :, WID:PAD] = jnp.zeros((2, ROWS, PAD - WID), BF)
         cols = slice(lo, lo + 256)
         for n, (src, dst) in enumerate(((act.at[:, cols], act_out.at[:, cols]), (mid.at[:, :, cols], mid_out.at[:, :, cols]))):
             stores.append(pltpu.make_async_copy(src, dst, out_sems.at[2 * c + n]))
@@ -243,46 +248,58 @@
 
 def back_body(
     got_hbm, wd_hbm, act_hbm, mid_hbm, wg_hbm, wu_hbm,
-    d_out, gg_ref, gu_ref, prob_ref, p_ref, a_ref, b_ref,
-    got, wd, act, mid, wg, wu, d, sems, out_sem,
+    gg_out, gu_out, prob_ref, a_ref, b_ref,
+    got, wd, act, mid, g, w, d, got_sems, sems, out_sems,
 ):
-    got_loads = copies([(got_hbm.at[8 * i : 8 * i + 8], got.at[8 * i : 8 * i + 8]) for i in range(4)], sems)
-    loads = copies(
-        [(wd_hbm.at[lo : lo + size, :], wd.at[lo : lo + size, :]) for lo, size in CHUNKS]
-        + [(mid_hbm, mid), (act_hbm, act), (wg_hbm.at[2], wg), (wu_hbm.at[2], wu)],
-        sems.at[4:],
-    )
+    eights = [slice(8 * i, 8 * i + 8) for i in range(OWNERS // 8)]
+    got_loads = copies([(got_hbm.at[part], got.at[part]) for part in eights], got_sems)
+    pairs = []
+    for lo, size in CHUNKS:
+        cols = slice(lo, lo + 256)
+        pairs += [
+            (wd_hbm.at[lo : lo + size, :], wd.at[lo : lo + size, :]),
+            (mid_hbm.at[:, :, cols], mid.at[:, :, cols]),
+        ]
+        if lo == 0:
+            pairs.append((act_hbm, act))
+    pairs += [(ref.at[2], w.at[PAD * n : PAD * n + WID, :]) for n, ref in enumerate((wg_hbm, wu_hbm))]
+    loads = copies(pairs[:3], sems)
 
     def store(row, lane, value):
         width = min(128, FEAT - lane)
         d[row : row + value.shape[0], lane : lane + width] = value[:, :width]
 
-    for i in range(4):
-        got_loads[i].wait()
-        unpack(got.at[8 * i : 8 * i + 8], FPAD, store, 8 * i)
-    keep_d = pltpu.make_async_copy(d, d_out, out_sem)
-    keep_d.start()
+    for part, copy in zip(eights, got_loads):
+        copy.wait()
+        unpack(got.at[part], FPAD, store, part.start)
+    loads += copies(pairs[3:], sems.at[3:])
+    for n in range(2):
+        w[PAD * n + WID : PAD * n + PAD, :] = jnp.zeros((PAD - WID, PAD), BF)
+        g[:, PAD * n + WID : PAD * n + PAD] = jnp.zeros((ROWS, PAD - WID), BF)
     total = jnp.zeros((ROWS, 1), F32)
     for c, (lo, size) in enumerate(CHUNKS):
-        loads[c].wait()
+        wait = loads[:3] if c == 0 else loads[2 * c + 1 : 2 * c + 3]
+        wait[0].wait()
         down_back = dot(d[...], wd[lo : lo + size, :], NT)
+        for copy in wait[1:]:
+            copy.wait()
         if c == 0:
-            loads[3].wait()
-            loads[4].wait()
-            p_col = mid[0, :, 640:768][:, WID - 640 : WID - 639]
-            p_ref[...] = p_col
+            p_col = act[:, 640:768].astype(F32)[:, PROB - 640 : PROB - 639]
         delta = p_col * down_back
-        gg_ref[:, lo : lo + size] = (delta * mid[0, :, lo : lo + size]).astype(BF)
-        gu_ref[:, lo : lo + size] = (delta * mid[1, :, lo : lo + size]).astype(BF)
+        g[:, lo : lo + size] = (delta * mid[0, :, lo : lo + size]).astype(BF)
+        g[:, PAD + lo : PAD + lo + size] = (delta * mid[1, :, lo : lo + size]).astype(BF)
         total = total + jnp.sum(act[:, lo : lo + size].astype(F32) * down_back, axis=1, keepdims=True)
-    prob_ref[...] = jnp.where(iota((ROWS, 128), 1) == PROB - 640, total, 0.0)
-    loads[5].wait()
-    loads[6].wait()
-    left, right = dx_of(gg_ref[...], gu_ref[...], wg[...], wu[...], prob_ref[...])
-    right = split_prob(right)
+    stores = copies([(g.at[:, 0:PAD], gg_out), (g.at[:, PAD : 2 * PAD], gu_out)], out_sems)
+    prob = jnp.where(iota((ROWS, 128), 1) == PROB - 640, total, 0.0)
+    prob_ref[...] = prob
+    loads[7].wait()
+    loads[8].wait()
+    val = dot(g[...], w[...], NN)
+    left, right = val[:, :640], split_prob(val[:, 640:768] + prob)
     put_rows(a_ref, left[:HALF], right[:HALF])
     put_rows(b_ref, left[HALF:], right[HALF:])
-    keep_d.wait()
+    for copy in stores:
+        copy.wait()
 
 
 def split_prob(tile):
@@ -302,7 +319,7 @@
 
 
 def dx_of(gg, gu, wg, wu, prob):
-    val = dot(gg, wg, NN) + dot(gu, wu, NN)
+    val = dot(gg[:, :WID], wg, NN) + dot(gu[:, :WID], wu, NN)
     return val[:, :640], val[:, 640:768] + prob
 
 
@@ -372,10 +389,16 @@
             out[:, WID * j : WID * j + WID] = dot(src[...], x, TN).astype(BF)[:, :WID]
 
 
-def down_body(d_ref, act_ref, p_ref, out_ref, scaled):
+def down_body(got, act_ref, act_tail_ref, out_ref, scaled):
     @pl.when(pl.program_id(0) == 0)
     def _():
-        scaled[...] = (d_ref[...].astype(F32) * p_ref[...]).astype(BF)
+        def store(row, lane, value):
+            width = min(128, FEAT - lane)
+            scaled[row : row + value.shape[0], lane : lane + width] = value[:, :width]
+
+        unpack(got, FPAD, store)
+        p_col = act_tail_ref[...].astype(F32)[:, PROB - 640 : PROB - 639]
+        scaled[...] = (scaled[...].astype(F32) * p_col).astype(BF)
 
     out_ref[...] = dot(act_ref[...], scaled[...], TN).astype(BF)
 
@@ -387,7 +410,7 @@
         grid=(3,),
         in_specs=[sm(), pl.BlockSpec((240, FEAT), lambda i: (i, 0))],
         out_specs=pl.BlockSpec((SIDES, 240, PAD), lambda i: (0, i, 0)),
-        vmem=60,
+        vmem=TURN_VMEM,
     )(t, w)
 
 
@@ -448,52 +471,55 @@
         out_specs=vm(),
         scratch_shapes=[pltpu.VMEM((3072, TOK), BF), pltpu.VMEM((ROWS - MROWS, FPAD), BF)],
         flops=2 * 10**9,
-        vmem=60,
+        vmem=SEND_VMEM,
     )(t, pick, d_t, d_below, d_above, d_far_a, d_far_b)
     got_d = lax.all_to_all(send_d, "dp", 0, 0, tiled=True)
     x_far_a, x_far_b = from_below(x_below_a), from_above(x_above_b)
     act_spec = pl.BlockSpec((ROWS, 256), lambda i: (0, i))
     row_spec = pl.BlockSpec((256, FEAT), lambda i: (i, 0))
-    mid = struct((ROWS, WID))
+    mid = struct((ROWS, PAD))
     half, half32 = struct((HALF, PAD)), struct((HALF, PAD), F32)
     act, fgu, x_rel = call(
         gate_up_body,
-        (struct((ROWS, PAD)), struct((2, ROWS, PAD), F32), struct((SIDES, ROWS, PAD))),
-        in_specs=[vm()] * 7 + [hbm()] * 2,
+        (struct((ROWS, PAD)), struct((2, ROWS, PAD)), struct((SIDES, ROWS, PAD))),
+        in_specs=[hbm()] * 9,
         out_specs=(hbm(),) * 3,
         scratch_shapes=[
+            pltpu.VMEM((SIDES, OWNERS, bx, 128), BF),
             pltpu.VMEM((2, SIDES, WID, PAD), BF),
             pltpu.VMEM((ROWS, PAD), BF),
-            pltpu.VMEM((2, ROWS, PAD), F32),
+            pltpu.VMEM((2, ROWS, PAD), BF),
             pltpu.VMEM((SIDES, ROWS, PAD), BF),
+            dma(7),
             dma(6),
             dma(7),
         ],
         flops=5 * 10**9,
         vmem=GATE_VMEM,
     )(got_x, x_below_a, x_below_b, x_above_a, x_above_b, x_far_a, x_far_b, wg, wu)
-    d_rows, gg, gu, prob, p_col, part_a, part_b = call(
+    gg, gu, prob, part_a, part_b = call(
         back_body,
-        (struct((ROWS, FEAT)), mid, mid, struct((ROWS, 128), F32), struct((ROWS, 1), F32), half, half),
+        (mid, mid, struct((ROWS, 128), F32), half, half),
         in_specs=[hbm()] * 6,
-        out_specs=(hbm(),) + (vm(),) * 6,
+        out_specs=(hbm(),) * 2 + (vm(),) * 3,
         scratch_shapes=[
             pltpu.VMEM((OWNERS, bd, 128), BF),
             pltpu.VMEM((WID, FEAT), BF),
             pltpu.VMEM((ROWS, PAD), BF),
-            pltpu.VMEM((2, ROWS, PAD), F32),
-            pltpu.VMEM((WID, PAD), BF),
-            pltpu.VMEM((WID, PAD), BF),
+            pltpu.VMEM((2, ROWS, PAD), BF),
+            pltpu.VMEM((ROWS, 2 * PAD), BF),
+            pltpu.VMEM((2 * PAD, PAD), BF),
             pltpu.VMEM((ROWS, FEAT), BF),
-            dma(11),
-            pltpu.SemaphoreType.DMA,
+            dma(4),
+            dma(9),
+            dma(2),
         ],
         flops=4 * 10**9,
         vmem=BACK_VMEM,
     )(got_d, wd, act, fgu, wg, wu)
     came_a, came_b = from_below(part_a), from_above(part_b)
     side = lambda k: pl.BlockSpec((1, WID, PAD), lambda i: (k, 0, 0))
-    acts = [whole((ROWS, WID))] * 2
+    acts = [whole((ROWS, PAD))] * 2
     tail = [whole((ROWS, 128))]
     send_a, send_b, keep_a, keep_b = call(
         near_dx_body,
@@ -502,7 +528,7 @@
         in_specs=acts + [side(1), side(1), side(3), side(3)] + tail,
         out_specs=(whole((HALF, PAD)),) * 4,
         flops=24 * 10**8,
-        vmem=20,
+        vmem=NEAR_VMEM,
     )(gg, gu, wg, wu, wg, wu, prob)
     below_b, above_a = from_below(send_a), from_above(send_b)
     own = call(
@@ -512,7 +538,7 @@
         in_specs=acts + [side(0), side(0)] + tail,
         out_specs=whole((ROWS, PAD)),
         flops=12 * 10**8,
-        vmem=20,
+        vmem=NEAR_VMEM,
     )(gg, gu, wg, wu, prob)
     pass_a, pass_b = call(relay_body, (half, half), in_specs=[vm()] * 4, out_specs=(vm(), vm()), vmem=10)(
         keep_a, came_a, keep_b, came_b
@@ -541,12 +567,12 @@
         down_body,
         struct((WID, FEAT)),
         grid=(3,),
-        in_specs=[whole((ROWS, FEAT)), act_spec, whole((ROWS, 1))],
+        in_specs=[whole((OWNERS, bd, 128)), act_spec, pl.BlockSpec((ROWS, 128), lambda i: (0, 5))],
         out_specs=row_spec,
         scratch_shapes=[pltpu.VMEM((ROWS, FEAT), BF)],
         flops=3 * 10**9,
         vmem=20,
-    )(d_rows, act, p_col)
+    )(got_d, act, act)
     dx_t, dp_t = call(
         combine_body,
         (struct((WID, TOK)), struct((TOP, TOK))),

time: 165 us -> 159 us (0.964)
  Pallas kernels: 72.8 us -> 70 us
  local copies, waits for them, and re-layouts: 8.4 us -> 6.57 us
  starting transfers between devices: 51.7 us -> 49.9 us
    unnamed x52 -> x42, local copies, waits for them, and re-layouts: 8.28 us -> 6.45 us
  transfers between devices with their start and end apart: 19 -> 19, of which waited for: 8 -> 8; matrix products, arithmetic and copies ran while one was open for 0% -> 0% of each run, Pallas kernels for 34% -> 35%
where the time goes in v1:
time: 159 us; the launch traced here: 158 us
  Pallas kernels  70 us (44%)
  starting transfers between devices  49.9 us (31%)
  waiting for transfers between devices  31.1 us (20%)
  local copies, waits for them, and re-layouts  6.57 us (4%)
    ppermute x8, starting transfers between devices, from_above(): return lax.ppermute(value, 'tensor', above)  20.8 us
    ppermute x8, waiting for transfers between devices, from_above(): return lax.ppermute(value, 'tensor', above)  14.5 us
    pallas_call x2, Pallas kernels, turn(): call(turn_body, struct((SIDES, WID, PAD)), grid=(3,), in_specs=[sm(), pl....  13.3 us
    pallas_call x1, Pallas kernels, shards(): call(back_body, (mid, mid, struct((ROWS, 128), F32), half, half), in_spec...  11.8 us
    pallas_call x1, Pallas kernels, shards(): call(gate_up_body, (struct((ROWS, PAD)), struct((2, ROWS, PAD)), struct((...  11.4 us
    pallas_call x1, Pallas kernels, shards(): call(grad_pair_body, (struct((WID, FEAT)), struct((WID, FEAT))), grid=(3,...  9.75 us
    all_to_all x1, starting transfers between devices, shards(): back = lax.all_to_all(send_back, 'dp', 0, 0, tiled=True)  9.61 us
    all_to_all x1, starting transfers between devices, shards(): got_x = lax.all_to_all(send_x, 'dp', 0, 0, tiled=True)  9.45 us
  transfers between devices with their start and end apart: 19, of which 8 were waited for; matrix products, arithmetic and copies ran while one was open for 0% of the time, Pallas kernels for 35%

profile of v1, /device:TPU:1, one launch (start us, length us, event | category | flops | bytes accessed | tf_op | source)
XLA Modules:
  0.0 158.5 jit_solution(3723280779213008516)
XLA Ops:
  0.6 2.1 %collective-permute-start = (bf16[720,384]{1,0:T(8,128)(2,1)}, bf16[720,384]{1,0:T(8,128)(2,1)S(1)}, u32[]{:S(2)}, u32[]{:S(2)}) collective-permute-start(bf16[720,384]{1,0:T(8,128)(2,1)} %bitcast.24), channel_id=1, source_target_pairs={{3,0},{0,1},{1,2},{2,3},{7,4},{4,5},{5,6},{6,7},{11,8},{8,9},{9,10... | collective-permute-start | bytes 1658888 | tf_op jit(solution)/shard_map/ppermute | solution.py:441
  2.7 1.3 collective-permute-start.1
  4.1 3.3 %shard_map.119 = (bf16[32,112,128]{2,1,0:T(8,128)(2,1)}, bf16[576,384]{1,0:T(8,128)(2,1)}) custom-call(s32[4,384]{1,0:T(4,128)} %bitcast.27, bf16[4,384]{1,0:T(4,128)(2,1)} %bitcast.35, s32[1,128]{1,0:T(1,128)} %bitcast.29, bf16[720,384]{1,0:T(8,128)(2,1)} %bitcast.34), custom_call_target="tpu_custom_call" | custom-call | flops 1000000000 | bytes 4194304 | tf_op jit(solution)/shard_map/pallas_call | solution.py:451
  7.4 9.4 %all-to-all-start.1 = ((bf16[32,112,128]{2,1,0:T(8,128)(2,1)}), bf16[32,112,128]{2,1,0:T(8,128)(2,1)S(1)}, u32[]{:S(2)}, u32[]{:S(2)}) async-start(bf16[32,112,128]{2,1,0:T(8,128)(2,1)} %get-tuple-element.34), calls=%async_computation.1 | async-start | bytes 1835008 | tf_op jit(solution)/shard_map/all_to_all | solution.py:460
  16.9 0.1 collective-permute-start.2
  17.0 0.0 collective-permute-done.1.above_ref
  17.1 2.7 %collective-permute-start.3 = (bf16[352,384]{1,0:T(8,128)(2,1)S(1)}, bf16[352,384]{1,0:T(8,128)(2,1)S(1)}, u32[]{:S(2)}, u32[]{:S(2)}) collective-permute-start(bf16[352,384]{1,0:T(8,128)(2,1)S(1)} %slice.17), channel_id=1, source_target_pairs={{1,0},{2,1},{3,2},{0,3},{5,4},{6,5},{7,6},{4,7},{9,8},{10,9},{11,1... | collective-permute-start | bytes 811016 | tf_op jit(solution)/shard_map/ppermute | solution.py:438
  19.8 4.7 %collective-permute-done.3.far_b_ref = bf16[352,384]{1,0:T(8,128)(2,1)S(1)} collective-permute-done((bf16[352,384]{1,0:T(8,128)(2,1)S(1)}, bf16[352,384]{1,0:T(8,128)(2,1)S(1)}, u32[]{:S(2)}, u32[]{:S(2)}) %collective-permute-start.3) | collective-permute-done | bytes 270368 | tf_op jit(solution)/shard_map/ppermute | solution.py:438
  24.5 1.2 collective-permute-done.2.far_a_ref
  25.7 1.0 copy-done.9
  26.7 4.1 %shard_map.120 = bf16[32,416,128]{2,1,0:T(8,128)(2,1)} custom-call(s32[1]{0:T(128)} %bitcast.t_ref, bf16[576,384]{1,0:T(8,128)(2,1)S(1)} %copy-done.9, bf16[720,384]{1,0:T(8,128)(2,1)S(1)} %bitcast.26, bf16[720,384]{1,0:T(8,128)(2,1)S(1)} %collective-permute-done.below_ref, bf16[720,384]{1,0:T(8,128)(2,1)S(1)} %collective-permute-done.1.above_ref, ...), custom_call_target="tpu_custom_call" | custom-call | flops 2000000000 | bytes 4194304 | tf_op jit(solution)/shard_map/pallas_call | solution.py:467
  30.8 1.7 %all-to-all-done.1.refs_0_ = bf16[32,112,128]{2,1,0:T(8,128)(2,1)S(1)} async-done(((bf16[32,112,128]{2,1,0:T(8,128)(2,1)}), bf16[32,112,128]{2,1,0:T(8,128)(2,1)S(1)}, u32[]{:S(2)}, u32[]{:S(2)}) %all-to-all-start.1) | async-done | bytes 917536 | tf_op jit(solution)/shard_map/all_to_all | solution.py:460
  32.5 7.6 %all-to-all-start = ((bf16[32,416,128]{2,1,0:T(8,128)(2,1)}), bf16[32,416,128]{2,1,0:T(8,128)(2,1)}, u32[]{:S(2)}, u32[]{:S(2)}) async-start(bf16[32,416,128]{2,1,0:T(8,128)(2,1)} %shard_map.120), calls=%async_computation | async-start | bytes 6815744 | tf_op jit(solution)/shard_map/all_to_all | solution.py:476
  40.1 0.1 fusion
  40.2 2.6 %collective-permute-start.7 = (bf16[16,112,128]{2,1,0:T(8,128)(2,1)S(1)}, bf16[16,112,128]{2,1,0:T(8,128)(2,1)S(1)}, u32[]{:S(2)}, u32[]{:S(2)}) collective-permute-start(bf16[16,112,128]{2,1,0:T(8,128)(2,1)S(1)} %get-tuple-element.57), channel_id=1, source_target_pairs={{1,0},{2,1},{3,2},{0,3},{5,4},{6,5},{7,6},{4,7},{9,8},{10,9},{11,1... | collective-permute-start | bytes 1376264 | tf_op jit(solution)/shard_map/ppermute | solution.py:438
  42.8 2.7 %collective-permute-start.6 = (bf16[16,112,128]{2,1,0:T(8,128)(2,1)S(1)}, bf16[16,112,128]{2,1,0:T(8,128)(2,1)S(1)}, u32[]{:S(2)}, u32[]{:S(2)}) collective-permute-start(bf16[16,112,128]{2,1,0:T(8,128)(2,1)S(1)} %get-tuple-element.58), channel_id=1, source_target_pairs={{1,0},{2,1},{3,2},{0,3},{5,4},{6,5},{7,6},{4,7},{9,8},{10,9},{11,1... | collective-permute-start | bytes 1376264 | tf_op jit(solution)/shard_map/ppermute | solution.py:438
  45.5 6.9 %collective-permute-done.7.refs_4_ = bf16[16,112,128]{2,1,0:T(8,128)(2,1)S(1)} collective-permute-done((bf16[16,112,128]{2,1,0:T(8,128)(2,1)S(1)}, bf16[16,112,128]{2,1,0:T(8,128)(2,1)S(1)}, u32[]{:S(2)}, u32[]{:S(2)}) %collective-permute-start.7) | collective-permute-done | bytes 458784 | tf_op jit(solution)/shard_map/ppermute | solution.py:438
  52.4 3.5 %collective-permute-start.9 = (bf16[16,112,128]{2,1,0:T(8,128)(2,1)S(1)}, bf16[16,112,128]{2,1,0:T(8,128)(2,1)S(1)}, u32[]{:S(2)}, u32[]{:S(2)}) collective-permute-start(bf16[16,112,128]{2,1,0:T(8,128)(2,1)S(1)} %collective-permute-done.7.refs_4_), channel_id=1, source_target_pairs={{1,0},{2,1},{3,2},{0,3},{5,4},{6,5},{7,6},{4,7},{9,8},{10,9},{11,1... | collective-permute-start | bytes 1376264 | tf_op jit(solution)/shard_map/ppermute | solution.py:438
  55.9 6.7 %shard_map.122.refs_8_.wu_hbm.wu_ref.wua_ref.wub_ref = bf16[4,720,768]{2,1,0:T(8,128)(2,1)} custom-call(s32[1]{0:T(128)} %bitcast.t_ref, bf16[720,2880]{1,0:T(8,128)(2,1)} %bitcast.31), custom_call_target="tpu_custom_call" | custom-call | bytes 4194304 | tf_op jit(solution)/shard_map/pallas_call | solution.py:407
  62.6 6.5 %shard_map.121.refs_7_.wg_hbm.wg_ref.wga_ref.wgb_ref = bf16[4,720,768]{2,1,0:T(8,128)(2,1)} custom-call(s32[1]{0:T(128)} %bitcast.t_ref, bf16[720,2880]{1,0:T(8,128)(2,1)} %bitcast.32), custom_call_target="tpu_custom_call" | custom-call | bytes 4194304 | tf_op jit(solution)/shard_map/pallas_call | solution.py:407
  69.2 2.8 %collective-permute-done.9.refs_6_ = bf16[16,112,128]{2,1,0:T(8,128)(2,1)S(1)} collective-permute-done((bf16[16,112,128]{2,1,0:T(8,128)(2,1)S(1)}, bf16[16,112,128]{2,1,0:T(8,128)(2,1)S(1)}, u32[]{:S(2)}, u32[]{:S(2)}) %collective-permute-start.9) | collective-permute-done | bytes 458784 | tf_op jit(solution)/shard_map/ppermute | solution.py:438
  72.0 3.2 %collective-permute-done.8.refs_5_ = bf16[16,112,128]{2,1,0:T(8,128)(2,1)S(1)} collective-permute-done((bf16[16,112,128]{2,1,0:T(8,128)(2,1)S(1)}, bf16[16,112,128]{2,1,0:T(8,128)(2,1)S(1)}, u32[]{:S(2)}, u32[]{:S(2)}) %collective-permute-start.8) | collective-permute-done | bytes 458784 | tf_op jit(solution)/shard_map/ppermute | solution.py:441
  75.3 0.8 copy-done.18
  76.1 11.4 %shard_map.123 = (bf16[576,768]{1,0:T(8,128)(2,1)}, bf16[2,576,768]{2,1,0:T(8,128)(2,1)}, bf16[4,576,768]{2,1,0:T(8,128)(2,1)}) custom-call(bf16[32,112,128]{2,1,0:T(8,128)(2,1)} %copy-done.12, bf16[16,112,128]{2,1,0:T(8,128)(2,1)} %copy-done.14, bf16[16,112,128]{2,1,0:T(8,128)(2,1)} %copy-done.15, bf16[16,112,128]{2,1,0:T(8,128)(2,1)} %copy-done.16, ...), custom_call_target="tpu_custom_call" | custom-call | flops 5000000000 | bytes 4194304 | tf_op jit(solution)/shard_map/pallas_call | solution.py:482
  87.5 11.8 %shard_map.124 = (bf16[576,768]{1,0:T(8,128)(2,1)}, bf16[576,768]{1,0:T(8,128)(2,1)}, f32[576,128]{1,0:T(8,128)S(1)}, bf16[288,768]{1,0:T(8,128)(2,1)S(1)}, bf16[288,768]{1,0:T(8,128)(2,1)S(1)}) custom-call(bf16[32,416,128]{2,1,0:T(8,128)(2,1)} %all-to-all-done.got_hbm.got, bf16[720,2880]{1,0:T(8,128)(2,1)} %bitcast.33, ...), custom_call_target="tpu_custom_call" | custom-call | flops 4000000000 | bytes 4194304 | tf_op jit(solution)/shard_map/pallas_call | solution.py:500
  99.2 0.1 collective-permute-start.10
  99.3 2.7 %collective-permute-start.11 = (bf16[288,768]{1,0:T(8,128)(2,1)S(1)}, bf16[288,768]{1,0:T(8,128)(2,1)S(1)}, u32[]{:S(2)}, u32[]{:S(2)}) collective-permute-start(bf16[288,768]{1,0:T(8,128)(2,1)S(1)} %get-tuple-element.43), channel_id=1, source_target_pairs={{1,0},{2,1},{3,2},{0,3},{5,4},{6,5},{7,6},{4,7},{9,8},{10,9},{11,1... | collective-permute-start | bytes 1327112 | tf_op jit(solution)/shard_map/ppermute | solution.py:438
  102.0 2.3 %copy-done = bf16[4,720,768]{2,1,0:T(8,128)(2,1)S(1)} copy-done((bf16[4,720,768]{2,1,0:T(8,128)(2,1)S(1)}, bf16[4,720,768]{2,1,0:T(8,128)(2,1)}, u32[]{:S(2)}) %copy-start) | copy-done | bytes 4423704
  104.2 1.2 copy-done.1
  105.4 1.2 copy-done.3
  106.6 2.9 %shard_map.126 = (bf16[288,768]{1,0:T(8,128)(2,1)S(1)}, bf16[288,768]{1,0:T(8,128)(2,1)S(1)}, f32[288,768]{1,0:T(8,128)S(1)}, f32[288,768]{1,0:T(8,128)S(1)}) custom-call(bf16[576,768]{1,0:T(8,128)(2,1)S(1)} %copy-done.1, bf16[576,768]{1,0:T(8,128)(2,1)S(1)} %copy-done.3, bf16[4,720,768]{2,1,0:T(8,128)(2,1)S(1)} %copy-done, ...), custom_call_target="tpu_custom_call" | custom-call | flops 2400000000 | bytes 4194304 | tf_op jit(solution)/shard_map/pallas_call | solution.py:524
  109.5 0.1 collective-permute-start.14
  109.6 0.0 copy-start.2
  109.6 0.0 copy-start.11
  109.6 2.6 %collective-permute-start.15 = (bf16[288,768]{1,0:T(8,128)(2,1)S(1)}, bf16[288,768]{1,0:T(8,128)(2,1)S(1)}, u32[]{:S(2)}, u32[]{:S(2)}) collective-permute-start(bf16[288,768]{1,0:T(8,128)(2,1)S(1)} %get-tuple-element.51), channel_id=1, source_target_pairs={{1,0},{2,1},{3,2},{0,3},{5,4},{6,5},{7,6},{4,7},{9,8},{10,9},{11,1... | collective-permute-start | bytes 1327112 | tf_op jit(solution)/shard_map/ppermute | solution.py:438
  112.3 1.5 shard_map.125.own_ref
  113.8 0.5 shard_map.127
  114.3 0.1 collective-permute-start.12
  114.4 2.7 %collective-permute-start.13 = (bf16[288,768]{1,0:T(8,128)(2,1)S(1)}, bf16[288,768]{1,0:T(8,128)(2,1)S(1)}, u32[]{:S(2)}, u32[]{:S(2)}) collective-permute-start(bf16[288,768]{1,0:T(8,128)(2,1)S(1)} %get-tuple-element.45), channel_id=1, source_target_pairs={{1,0},{2,1},{3,2},{0,3},{5,4},{6,5},{7,6},{4,7},{9,8},{10,9},{11,1... | collective-permute-start | bytes 1327112 | tf_op jit(solution)/shard_map/ppermute | solution.py:438
  117.1 9.7 %shard_map.128 = (bf16[720,2880]{1,0:T(8,128)(2,1)}, bf16[720,2880]{1,0:T(8,128)(2,1)}) custom-call(s32[1]{0:T(128)} %bitcast.t_ref, bf16[4,576,768]{2,1,0:T(8,128)(2,1)S(1)} %copy-done.11, bf16[576,768]{1,0:T(8,128)(2,1)S(1)} %copy-done.2, bf16[576,768]{1,0:T(8,128)(2,1)S(1)} %copy-done.4), custom_call_target="tpu_custom_call" | custom-call | flops 5000000000 | bytes 4194304 | tf_op jit(solution)/shard_map/pallas_call | solution.py:547
  126.9 3.2 %collective-permute-done.12.below_a = bf16[288,768]{1,0:T(8,128)(2,1)S(1)} collective-permute-done((bf16[288,768]{1,0:T(8,128)(2,1)S(1)}, bf16[288,768]{1,0:T(8,128)(2,1)S(1)}, u32[]{:S(2)}, u32[]{:S(2)}) %collective-permute-start.12) | collective-permute-done | bytes 442400 | tf_op jit(solution)/shard_map/ppermute | solution.py:441
  130.1 1.4 shard_map.129
  131.5 9.6 %all-to-all-start.2 = ((bf16[32,112,128]{2,1,0:T(8,128)(2,1)}), bf16[32,112,128]{2,1,0:T(8,128)(2,1)S(1)}, u32[]{:S(2)}, u32[]{:S(2)}) async-start(bf16[32,112,128]{2,1,0:T(8,128)(2,1)} %shard_map.129), calls=%async_computation.2 | async-start | bytes 1835008 | tf_op jit(solution)/shard_map/all_to_all | solution.py:565
  141.1 0.0 copy-start.7
  141.1 0.0 copy-start.8
  141.2 8.4 %shard_map.131 = bf16[720,2880]{1,0:T(8,128)(2,1)} custom-call(bf16[32,416,128]{2,1,0:T(8,128)(2,1)} %all-to-all-done.got_hbm.got, bf16[576,768]{1,0:T(8,128)(2,1)S(1)} %copy-done.5, bf16[576,768]{1,0:T(8,128)(2,1)S(1)} %copy-done.5), custom_call_target="tpu_custom_call" | custom-call | flops 3000000000 | bytes 4194304 | tf_op jit(solution)/shard_map/pallas_call | solution.py:566
  149.5 7.2 %all-to-all-done.2.back_ref = bf16[32,112,128]{2,1,0:T(8,128)(2,1)S(1)} async-done(((bf16[32,112,128]{2,1,0:T(8,128)(2,1)}), bf16[32,112,128]{2,1,0:T(8,128)(2,1)S(1)}, u32[]{:S(2)}, u32[]{:S(2)}) %all-to-all-start.2) | async-done | bytes 917536 | tf_op jit(solution)/shard_map/all_to_all | solution.py:565
  156.8 1.7 %shard_map.130 = (bf16[720,384]{1,0:T(8,128)(2,1)}, bf16[4,384]{1,0:T(4,128)(2,1)}) custom-call(bf16[32,112,128]{2,1,0:T(8,128)(2,1)S(1)} %all-to-all-done.2.back_ref, bf16[576,384]{1,0:T(8,128)(2,1)S(1)} %copy-done.10, s32[4,384]{1,0:T(4,128)S(1)} %bitcast.28, s32[1,128]{1,0:T(1,128)S(1)} %bitcast.30), custom_call_target="tpu_custom_call" | custom-call | flops 1000000000 | bytes 4194304 | tf_op jit(solution)/shard_map/pallas_call | solution.py:576
  (49 shorter events, 0.2 us)
Async XLA Ops:
  0.6 25.0 %copy-start.6 = (bf16[384,720]{0,1:T(8,128)(2,1)S(1)}, bf16[384,720]{0,1:T(8,128)(2,1)}, u32[]{:S(2)}) copy-start(bf16[384,720]{0,1:T(8,128)(2,1)} %param.9) | copy-start | bytes 1658884
  0.6 16.2 %collective-permute-start = (bf16[720,384]{1,0:T(8,128)(2,1)}, bf16[720,384]{1,0:T(8,128)(2,1)S(1)}, u32[]{:S(2)}, u32[]{:S(2)}) collective-permute-start(bf16[720,384]{1,0:T(8,128)(2,1)} %bitcast.24), channel_id=1, source_target_pairs={{3,0},{0,1},{1,2},{2,3},{7,4},{4,5},{5,6},{6,7},{11,8},{8,9},{9,10... | collective-permute-start | bytes 1658888 | tf_op jit(solution)/shard_map/ppermute | solution.py:441
  2.7 14.3 %collective-permute-start.1 = (bf16[720,384]{1,0:T(8,128)(2,1)}, bf16[720,384]{1,0:T(8,128)(2,1)S(1)}, u32[]{:S(2)}, u32[]{:S(2)}) collective-permute-start(bf16[720,384]{1,0:T(8,128)(2,1)} %bitcast.25), channel_id=1, source_target_pairs={{1,0},{2,1},{3,2},{0,3},{5,4},{6,5},{7,6},{4,7},{9,8},{10,9},{11,1... | collective-permute-start | bytes 1658888 | tf_op jit(solution)/shard_map/ppermute | solution.py:438
  7.4 25.1 %all-to-all-start.1 = ((bf16[32,112,128]{2,1,0:T(8,128)(2,1)}), bf16[32,112,128]{2,1,0:T(8,128)(2,1)S(1)}, u32[]{:S(2)}, u32[]{:S(2)}) async-start(bf16[32,112,128]{2,1,0:T(8,128)(2,1)} %get-tuple-element.34), calls=%async_computation.1 | async-start | bytes 1835008 | tf_op jit(solution)/shard_map/all_to_all | solution.py:460
  16.9 8.8 %collective-permute-start.2 = (bf16[368,384]{1,0:T(8,128)(2,1)S(1)}, bf16[368,384]{1,0:T(8,128)(2,1)S(1)}, u32[]{:S(2)}, u32[]{:S(2)}) collective-permute-start(bf16[368,384]{1,0:T(8,128)(2,1)S(1)} %slice.16), channel_id=1, source_target_pairs={{3,0},{0,1},{1,2},{2,3},{7,4},{4,5},{5,6},{6,7},{11,8},{8,9},{9,10... | collective-permute-start | bytes 847880 | tf_op jit(solution)/shard_map/ppermute | solution.py:441
  17.1 7.5 %collective-permute-start.3 = (bf16[352,384]{1,0:T(8,128)(2,1)S(1)}, bf16[352,384]{1,0:T(8,128)(2,1)S(1)}, u32[]{:S(2)}, u32[]{:S(2)}) collective-permute-start(bf16[352,384]{1,0:T(8,128)(2,1)S(1)} %slice.17), channel_id=1, source_target_pairs={{1,0},{2,1},{3,2},{0,3},{5,4},{6,5},{7,6},{4,7},{9,8},{10,9},{11,1... | collective-permute-start | bytes 811016 | tf_op jit(solution)/shard_map/ppermute | solution.py:438
  25.7 1.0 copy-start.9
  32.5 7.7 %copy-start.12 = (bf16[32,112,128]{2,1,0:T(8,128)(2,1)}, bf16[32,112,128]{2,1,0:T(8,128)(2,1)S(1)}, u32[]{:S(2)}) copy-start(bf16[32,112,128]{2,1,0:T(8,128)(2,1)S(1)} %all-to-all-done.1.refs_0_) | copy-start | bytes 2752516
  32.5 54.9 %all-to-all-start = ((bf16[32,416,128]{2,1,0:T(8,128)(2,1)}), bf16[32,416,128]{2,1,0:T(8,128)(2,1)}, u32[]{:S(2)}, u32[]{:S(2)}) async-start(bf16[32,416,128]{2,1,0:T(8,128)(2,1)} %shard_map.120), calls=%async_computation | async-start | bytes 6815744 | tf_op jit(solution)/shard_map/all_to_all | solution.py:476
  40.2 12.2 %collective-permute-start.7 = (bf16[16,112,128]{2,1,0:T(8,128)(2,1)S(1)}, bf16[16,112,128]{2,1,0:T(8,128)(2,1)S(1)}, u32[]{:S(2)}, u32[]{:S(2)}) collective-permute-start(bf16[16,112,128]{2,1,0:T(8,128)(2,1)S(1)} %get-tuple-element.57), channel_id=1, source_target_pairs={{1,0},{2,1},{3,2},{0,3},{5,4},{6,5},{7,6},{4,7},{9,8},{10,9},{11,1... | collective-permute-start | bytes 1376264 | tf_op jit(solution)/shard_map/ppermute | solution.py:438
  42.8 13.1 %collective-permute-start.4 = (bf16[16,112,128]{2,1,0:T(8,128)(2,1)S(1)}, bf16[16,112,128]{2,1,0:T(8,128)(2,1)S(1)}, u32[]{:S(2)}, u32[]{:S(2)}) collective-permute-start(bf16[16,112,128]{2,1,0:T(8,128)(2,1)S(1)} %get-tuple-element.58), channel_id=1, source_target_pairs={{3,0},{0,1},{1,2},{2,3},{7,4},{4,5},{5,6},{6,7},{11,8},{8,9},{9,10... | collective-permute-start | bytes 1376264 | tf_op jit(solution)/shard_map/ppermute | solution.py:441
  42.8 26.4 %collective-permute-start.5 = (bf16[16,112,128]{2,1,0:T(8,128)(2,1)S(1)}, bf16[16,112,128]{2,1,0:T(8,128)(2,1)S(1)}, u32[]{:S(2)}, u32[]{:S(2)}) collective-permute-start(bf16[16,112,128]{2,1,0:T(8,128)(2,1)S(1)} %get-tuple-element.57), channel_id=1, source_target_pairs={{3,0},{0,1},{1,2},{2,3},{7,4},{4,5},{5,6},{6,7},{11,8},{8,9},{9,10... | collective-permute-start | bytes 1376264 | tf_op jit(solution)/shard_map/ppermute | solution.py:441
  42.8 26.4 %collective-permute-start.6 = (bf16[16,112,128]{2,1,0:T(8,128)(2,1)S(1)}, bf16[16,112,128]{2,1,0:T(8,128)(2,1)S(1)}, u32[]{:S(2)}, u32[]{:S(2)}) collective-permute-start(bf16[16,112,128]{2,1,0:T(8,128)(2,1)S(1)} %get-tuple-element.58), channel_id=1, source_target_pairs={{1,0},{2,1},{3,2},{0,3},{5,4},{6,5},{7,6},{4,7},{9,8},{10,9},{11,1... | collective-permute-start | bytes 1376264 | tf_op jit(solution)/shard_map/ppermute | solution.py:438
  52.4 10.3 %copy-start.13 = (bf16[16,112,128]{2,1,0:T(8,128)(2,1)}, bf16[16,112,128]{2,1,0:T(8,128)(2,1)S(1)}, u32[]{:S(2)}) copy-start(bf16[16,112,128]{2,1,0:T(8,128)(2,1)S(1)} %collective-permute-done.7.refs_4_) | copy-start | bytes 1376260
  52.4 19.7 %collective-permute-start.9 = (bf16[16,112,128]{2,1,0:T(8,128)(2,1)S(1)}, bf16[16,112,128]{2,1,0:T(8,128)(2,1)S(1)}, u32[]{:S(2)}, u32[]{:S(2)}) collective-permute-start(bf16[16,112,128]{2,1,0:T(8,128)(2,1)S(1)} %collective-permute-done.7.refs_4_), channel_id=1, source_target_pairs={{1,0},{2,1},{3,2},{0,3},{5,4},{6,5},{7,6},{4,7},{9,8},{10,9},{11,1... | collective-permute-start | bytes 1376264 | tf_op jit(solution)/shard_map/ppermute | solution.py:438
  55.9 6.7 %copy-start.14 = (bf16[16,112,128]{2,1,0:T(8,128)(2,1)}, bf16[16,112,128]{2,1,0:T(8,128)(2,1)S(1)}, u32[]{:S(2)}) copy-start(bf16[16,112,128]{2,1,0:T(8,128)(2,1)S(1)} %collective-permute-done.4.refs_1_) | copy-start | bytes 1376260
  55.9 19.4 %collective-permute-start.8 = (bf16[16,112,128]{2,1,0:T(8,128)(2,1)S(1)}, bf16[16,112,128]{2,1,0:T(8,128)(2,1)S(1)}, u32[]{:S(2)}, u32[]{:S(2)}) collective-permute-start(bf16[16,112,128]{2,1,0:T(8,128)(2,1)S(1)} %collective-permute-done.4.refs_1_), channel_id=1, source_target_pairs={{3,0},{0,1},{1,2},{2,3},{7,4},{4,5},{5,6},{6,7},{11,8},{8,9},{9,10... | collective-permute-start | bytes 1376264 | tf_op jit(solution)/shard_map/ppermute | solution.py:441
  69.2 6.1 %copy-start.15 = (bf16[16,112,128]{2,1,0:T(8,128)(2,1)}, bf16[16,112,128]{2,1,0:T(8,128)(2,1)S(1)}, u32[]{:S(2)}) copy-start(bf16[16,112,128]{2,1,0:T(8,128)(2,1)S(1)} %collective-permute-done.5.refs_2_) | copy-start | bytes 1376260
  69.2 6.1 %copy-start.16 = (bf16[16,112,128]{2,1,0:T(8,128)(2,1)}, bf16[16,112,128]{2,1,0:T(8,128)(2,1)S(1)}, u32[]{:S(2)}) copy-start(bf16[16,112,128]{2,1,0:T(8,128)(2,1)S(1)} %collective-permute-done.6.refs_3_) | copy-start | bytes 1376260
  72.0 3.2 %copy-start.17 = (bf16[16,112,128]{2,1,0:T(8,128)(2,1)}, bf16[16,112,128]{2,1,0:T(8,128)(2,1)S(1)}, u32[]{:S(2)}) copy-start(bf16[16,112,128]{2,1,0:T(8,128)(2,1)S(1)} %collective-permute-done.9.refs_6_) | copy-start | bytes 1376260
  75.3 0.8 copy-start.18
  76.1 25.9 %slice-start = ((s8[4423680]{0:T(1024)(128)(4,1)}), s8[229376]{0:T(1024)(128)(4,1)S(1)}, s32[]{:S(2)}) async-start(s8[4423680]{0:T(1024)(128)(4,1)} %bitcast.22), calls=%async_computation.3 | async-start | bytes 458752
  87.5 14.5 %slice-start.1 = ((s8[4423680]{0:T(1024)(128)(4,1)}), s8[4194304]{0:T(1024)(128)(4,1)S(1)}, s32[]{:S(2)}) async-start(s8[4423680]{0:T(1024)(128)(4,1)} %bitcast.22), calls=%async_computation.4 | async-start | bytes 8388608
  99.2 14.6 %collective-permute-start.10 = (bf16[288,768]{1,0:T(8,128)(2,1)S(1)}, bf16[288,768]{1,0:T(8,128)(2,1)S(1)}, u32[]{:S(2)}, u32[]{:S(2)}) collective-permute-start(bf16[288,768]{1,0:T(8,128)(2,1)S(1)} %get-tuple-element.41), channel_id=1, source_target_pairs={{3,0},{0,1},{1,2},{2,3},{7,4},{4,5},{5,6},{6,7},{11,8},{8,9},{9,10... | collective-permute-start | bytes 1327112 | tf_op jit(solution)/shard_map/ppermute | solution.py:441
  99.3 14.5 %collective-permute-start.11 = (bf16[288,768]{1,0:T(8,128)(2,1)S(1)}, bf16[288,768]{1,0:T(8,128)(2,1)S(1)}, u32[]{:S(2)}, u32[]{:S(2)}) collective-permute-start(bf16[288,768]{1,0:T(8,128)(2,1)S(1)} %get-tuple-element.43), channel_id=1, source_target_pairs={{1,0},{2,1},{3,2},{0,3},{5,4},{6,5},{7,6},{4,7},{9,8},{10,9},{11,1... | collective-permute-start | bytes 1327112 | tf_op jit(solution)/shard_map/ppermute | solution.py:438
  102.0 2.3 %copy-start = (bf16[4,720,768]{2,1,0:T(8,128)(2,1)S(1)}, bf16[4,720,768]{2,1,0:T(8,128)(2,1)}, u32[]{:S(2)}) copy-start(bf16[4,720,768]{2,1,0:T(8,128)(2,1)} %shard_map.121.refs_7_.wg_hbm.wg_ref.wga_ref.wgb_ref) | copy-start | bytes 13271044
  104.2 1.2 copy-start.1
  105.4 1.2 copy-start.3
  106.6 5.7 %copy-start.4 = (bf16[576,768]{1,0:T(8,128)(2,1)S(1)}, bf16[576,768]{1,0:T(8,128)(2,1)}, u32[]{:S(2)}) copy-start(bf16[576,768]{1,0:T(8,128)(2,1)} %get-tuple-element.38.gu_ref) | copy-start | bytes 2654212
  109.5 20.6 %collective-permute-start.14 = (bf16[288,768]{1,0:T(8,128)(2,1)S(1)}, bf16[288,768]{1,0:T(8,128)(2,1)S(1)}, u32[]{:S(2)}, u32[]{:S(2)}) collective-permute-start(bf16[288,768]{1,0:T(8,128)(2,1)S(1)} %get-tuple-element.50), channel_id=1, source_target_pairs={{3,0},{0,1},{1,2},{2,3},{7,4},{4,5},{5,6},{6,7},{11,8},{8,9},{9,10... | collective-permute-start | bytes 1327112 | tf_op jit(solution)/shard_map/ppermute | solution.py:441
  109.6 7.5 %copy-start.2 = (bf16[576,768]{1,0:T(8,128)(2,1)S(1)}, bf16[576,768]{1,0:T(8,128)(2,1)}, u32[]{:S(2)}) copy-start(bf16[576,768]{1,0:T(8,128)(2,1)} %get-tuple-element.37.gg_ref) | copy-start | bytes 2654212
  109.6 7.5 %copy-start.11 = (bf16[4,576,768]{2,1,0:T(8,128)(2,1)S(1)}, bf16[4,576,768]{2,1,0:T(8,128)(2,1)}, u32[]{:S(2)}) copy-start(bf16[4,576,768]{2,1,0:T(8,128)(2,1)} %get-tuple-element.46.x_ref) | copy-start | bytes 10616836
  109.6 20.5 %collective-permute-start.15 = (bf16[288,768]{1,0:T(8,128)(2,1)S(1)}, bf16[288,768]{1,0:T(8,128)(2,1)S(1)}, u32[]{:S(2)}, u32[]{:S(2)}) collective-permute-start(bf16[288,768]{1,0:T(8,128)(2,1)S(1)} %get-tuple-element.51), channel_id=1, source_target_pairs={{1,0},{2,1},{3,2},{0,3},{5,4},{6,5},{7,6},{4,7},{9,8},{10,9},{11,1... | collective-permute-start | bytes 1327112 | tf_op jit(solution)/shard_map/ppermute | solution.py:438
  114.3 15.7 %collective-permute-start.12 = (bf16[288,768]{1,0:T(8,128)(2,1)S(1)}, bf16[288,768]{1,0:T(8,128)(2,1)S(1)}, u32[]{:S(2)}, u32[]{:S(2)}) collective-permute-start(bf16[288,768]{1,0:T(8,128)(2,1)S(1)} %get-tuple-element.44), channel_id=1, source_target_pairs={{3,0},{0,1},{1,2},{2,3},{7,4},{4,5},{5,6},{6,7},{11,8},{8,9},{9,10... | collective-permute-start | bytes 1327112 | tf_op jit(solution)/shard_map/ppermute | solution.py:441
  114.4 15.7 %collective-permute-start.13 = (bf16[288,768]{1,0:T(8,128)(2,1)S(1)}, bf16[288,768]{1,0:T(8,128)(2,1)S(1)}, u32[]{:S(2)}, u32[]{:S(2)}) collective-permute-start(bf16[288,768]{1,0:T(8,128)(2,1)S(1)} %get-tuple-element.45), channel_id=1, source_target_pairs={{1,0},{2,1},{3,2},{0,3},{5,4},{6,5},{7,6},{4,7},{9,8},{10,9},{11,1... | collective-permute-start | bytes 1327112 | tf_op jit(solution)/shard_map/ppermute | solution.py:438
  126.8 14.3 %copy-start.5 = (bf16[576,768]{1,0:T(8,128)(2,1)S(1)}, bf16[576,768]{1,0:T(8,128)(2,1)}, u32[]{:S(2)}) copy-start(bf16[576,768]{1,0:T(8,128)(2,1)} %get-tuple-element.35.act_hbm.act_ref.act_tail_ref) | copy-start | bytes 2654212
  131.5 25.3 %all-to-all-start.2 = ((bf16[32,112,128]{2,1,0:T(8,128)(2,1)}), bf16[32,112,128]{2,1,0:T(8,128)(2,1)S(1)}, u32[]{:S(2)}, u32[]{:S(2)}) async-start(bf16[32,112,128]{2,1,0:T(8,128)(2,1)} %shard_map.129), calls=%async_computation.2 | async-start | bytes 1835008 | tf_op jit(solution)/shard_map/all_to_all | solution.py:565
  141.1 15.6 %copy-start.7 = (s32[384,4]{0,1:T(4,128)S(1)}, s32[384,4]{0,1:T(4,128)}, u32[]{:S(2)}) copy-start(s32[384,4]{0,1:T(4,128)} %param.11) | copy-start | bytes 18436
  141.1 15.6 %copy-start.8 = (s32[128]{0:T(128)S(1)}, s32[128]{0:T(128)}, u32[]{:S(2)}) copy-start(s32[128]{0:T(128)} %param.12) | copy-start | bytes 1540
  141.1 15.6 %copy-start.10 = (bf16[576,384]{1,0:T(8,128)(2,1)S(1)}, bf16[576,384]{1,0:T(8,128)(2,1)}, u32[]{:S(2)}) copy-start(bf16[576,384]{1,0:T(8,128)(2,1)} %get-tuple-element.32.pick_ref) | copy-start | bytes 1327108

commit v2 on v1

--- a/solution.py
+++ b/solution.py
@@ -202,31 +202,63 @@
     return out
 
 
-def gate_up_body(*refs):
-    x_refs, w_refs, (act_out, mid_out, x_out), (got, w, act, mid, x, got_sems, in_sems, out_sems) = refs[:7], refs[7:9], refs[9:12], refs[12:]
-    peers = [slice(0, OWNERS)] + [slice(0, OWNERS // 2), slice(OWNERS // 2, OWNERS)] * 3
-    sides = [0, 3, 3, 1, 1, 2, 2]
-    blocks = [got.at[side, part] for side, part in zip(sides, peers)]
+def keep_side(x, side):
+    def store(row, lane, value):
+        x[side, row : row + value.shape[0], lane : lane + 128] = value
+
+    return store
+
+
+def gate_up_near_body(*refs):
+    x_refs, w_refs, (part_out, x_out), (got, w, part, x, got_sems, in_sems, out_sems) = refs[:5], refs[5:7], refs[7:9], refs[9:]
+    peers = [slice(0, OWNERS)] + [slice(0, OWNERS // 2), slice(OWNERS // 2, OWNERS)] * 2
+    places = [0, 2, 2, 1, 1]
+    blocks = [got.at[place, part_of] for place, part_of in zip(places, peers)]
     got_loads = copies(list(zip(x_refs, blocks)), got_sems)
-    pairs = [(w_refs[n].at[:, lo : lo + size, :], w.at[n, :, lo : lo + size, :]) for lo, size in CHUNKS for n in range(2)]
-    loads = copies(pairs[:2], in_sems)
-
-    def keep(side):
-        def store(row, lane, value):
-            x[side, row : row + value.shape[0], lane : lane + 128] = value
-
-        return store
-
-    for n, (side, part) in enumerate(zip(sides, peers)):
+    pairs = []
+    for lo, size in CHUNKS:
+        for n in range(2):
+            pairs.append((w_refs[n].at[0:2, lo : lo + size, :], w.at[n, 0:2, lo : lo + size, :]))
+            pairs.append((w_refs[n].at[3, lo : lo + size, :], w.at[n, 2, lo : lo + size, :]))
+    loads = copies(pairs[:4], in_sems)
+    for n, (place, part_of) in enumerate(zip(places, peers)):
         got_loads[n].wait()
-        unpack(blocks[n], PAD, keep(side), part.start)
-    loads += copies(pairs[2:], in_sems.at[2:])
-    stores = [pltpu.make_async_copy(x, x_out, out_sems.at[6])]
-    stores[0].start()
+        unpack(blocks[n], PAD, keep_side(x, place), part_of.start)
+    loads += copies(pairs[4:], in_sems.at[4:])
+    stores = copies([(x.at[0:2], x_out.at[0:2]), (x.at[2], x_out.at[3])], out_sems.at[3:])
     for c, (lo, size) in enumerate(CHUNKS):
-        loads[2 * c].wait()
-        loads[2 * c + 1].wait()
-        gate, up1 = (sum(dot(x[k], w[n, k, lo : lo + size, :], NT) for k in range(SIDES)) for n in range(2))
+        for copy in loads[4 * c : 4 * c + 4]:
+            copy.wait()
+        for n in range(2):
+            part[n, :, lo : lo + size] = sum(dot(x[k], w[n, k, lo : lo + size, :], NT) for k in range(3))
+        if c == 2:
+            tile = x[0, :, 640:768].astype(F32)
+            p_col = jnp.sum(jnp.where(iota((ROWS, 128), 1) == PROB - 640, tile, 0.0), axis=1, keepdims=True)
+            part[0, :, WID:PAD] = jnp.broadcast_to(p_col, (ROWS, PAD - WID))
+            part[1, :, WID:PAD] = jnp.zeros((ROWS, PAD - WID), F32)
+        stores += copies([(part.at[:, :, lo : lo + 256], part_out.at[:, :, lo : lo + 256])], out_sems.at[c : c + 1])
+    for copy in stores:
+        copy.wait()
+
+
+def gate_up_far_body(*refs):
+    x_refs, part_hbm, w_refs, (act_out, mid_out, x_out), scratch = refs[:2], refs[2], refs[3:5], refs[6:9], refs[9:]
+    got, w, part, act, mid, x, got_sems, in_sems, out_sems = scratch
+    blocks = [got.at[0 : OWNERS // 2], got.at[OWNERS // 2 : OWNERS]]
+    got_loads = copies(list(zip(x_refs, blocks)), got_sems)
+    pairs = []
+    for lo, size in CHUNKS:
+        pairs += [(w_refs[n].at[2, lo : lo + size, :], w.at[n, lo : lo + size, :]) for n in range(2)]
+        pairs.append((part_hbm.at[:, :, lo : lo + 256], part.at[:, :, lo : lo + 256]))
+    loads = copies(pairs, in_sems)
+    for n in range(2):
+        got_loads[n].wait()
+        unpack(blocks[n], PAD, keep_side(x, 0), n * OWNERS // 2)
+    stores = copies([(x.at[0], x_out.at[2])], out_sems.at[6:])
+    for c, (lo, size) in enumerate(CHUNKS):
+        for copy in loads[3 * c : 3 * c + 3]:
+            copy.wait()
+        gate, up1 = (part[n, :, lo : lo + size] + dot(x[0], w[n, lo : lo + size, :], NT) for n in range(2))
         up1 = up1 + 1.0
         sig = 1.0 / (1.0 + jnp.exp(-SWISH_SLOPE * gate))
         glu = gate * sig
@@ -234,14 +266,12 @@
         mid[0, :, lo : lo + size] = (up1 * (sig + SWISH_SLOPE * glu * (1.0 - sig))).astype(BF)
         mid[1, :, lo : lo + size] = glu.astype(BF)
         if c == 2:
-            tile = x[0, :, 640:768].astype(F32)
-            p_col = jnp.sum(jnp.where(iota((ROWS, 128), 1) == PROB - 640, tile, 0.0), axis=1, keepdims=True)
-            act[:, WID:PAD] = jnp.broadcast_to(p_col, (ROWS, PAD - WID)).astype(BF)
+            act[:, WID:PAD] = part[0, :, WID:PAD].astype(BF)
             mid[:, :, WID:PAD] = jnp.zeros((2, ROWS, PAD - WID), BF)
         cols = slice(lo, lo + 256)
-        for n, (src, dst) in enumerate(((act.at[:, cols], act_out.at[:, cols]), (mid.at[:, :, cols], mid_out.at[:, :, cols]))):
-            stores.append(pltpu.make_async_copy(src, dst, out_sems.at[2 * c + n]))
-            stores[-1].start()
+        stores += copies(
+            [(act.at[:, cols], act_out.at[:, cols]), (mid.at[:, :, cols], mid_out.at[:, :, cols])], out_sems.at[2 * c : 2 * c + 2]
+        )
     for copy in stores:
         copy.wait()
 
@@ -479,24 +509,43 @@
     row_spec = pl.BlockSpec((256, FEAT), lambda i: (i, 0))
     mid = struct((ROWS, PAD))
     half, half32 = struct((HALF, PAD)), struct((HALF, PAD), F32)
+    part, x_near = call(
+        gate_up_near_body,
+        (struct((2, ROWS, PAD), F32), struct((SIDES, ROWS, PAD))),
+        in_specs=[hbm()] * 7,
+        out_specs=(hbm(),) * 2,
+        scratch_shapes=[
+            pltpu.VMEM((3, OWNERS, bx, 128), BF),
+            pltpu.VMEM((2, 3, WID, PAD), BF),
+            pltpu.VMEM((2, ROWS, PAD), F32),
+            pltpu.VMEM((3, ROWS, PAD), BF),
+            dma(5),
+            dma(12),
+            dma(5),
+        ],
+        flops=4 * 10**9,
+        vmem=GATE_VMEM,
+    )(got_x, x_below_a, x_below_b, x_above_a, x_above_b, wg, wu)
     act, fgu, x_rel = call(
-        gate_up_body,
+        gate_up_far_body,
         (struct((ROWS, PAD)), struct((2, ROWS, PAD)), struct((SIDES, ROWS, PAD))),
-        in_specs=[hbm()] * 9,
+        in_specs=[hbm()] * 6,
         out_specs=(hbm(),) * 3,
+        input_output_aliases={5: 2},
         scratch_shapes=[
-            pltpu.VMEM((SIDES, OWNERS, bx, 128), BF),
-            pltpu.VMEM((2, SIDES, WID, PAD), BF),
+            pltpu.VMEM((OWNERS, bx, 128), BF),
+            pltpu.VMEM((2, WID, PAD), BF),
+            pltpu.VMEM((2, ROWS, PAD), F32),
             pltpu.VMEM((ROWS, PAD), BF),
             pltpu.VMEM((2, ROWS, PAD), BF),
-            pltpu.VMEM((SIDES, ROWS, PAD), BF),
-            dma(7),
-            dma(6),
+            pltpu.VMEM((1, ROWS, PAD), BF),
+            dma(2),
+            dma(9),
             dma(7),
         ],
-        flops=5 * 10**9,
+        flops=15 * 10**8,
         vmem=GATE_VMEM,
-    )(got_x, x_below_a, x_below_b, x_above_a, x_above_b, x_far_a, x_far_b, wg, wu)
+    )(x_far_a, x_far_b, part, wg, wu, x_near)
     gg, gu, prob, part_a, part_b = call(
         back_body,
         (mid, mid, struct((ROWS, 128), F32), half, half),

time: 159 us -> 159 us (level)
  waiting for transfers between devices: 31.1 us -> 24.3 us
  Pallas kernels: 70 us -> 74.3 us
  local copies, waits for them, and re-layouts: 6.57 us -> 8.21 us
    pallas_call x1 -> x2, Pallas kernels: 11.4 us -> 15.7 us  [the longest x1 9.2 us: shards(): call(gate_up_near_body, (struct((2, ROWS, PAD), F32), struct((SIDES, ROWS...]
    ppermute x8, waiting for transfers between devices: 7.66 us -> 3.68 us  [from_below(): return lax.ppermute(value, 'tensor', below)]
    ppermute x8, waiting for transfers between devices: 14.5 us -> 11.6 us  [from_above(): return lax.ppermute(value, 'tensor', above)]
    unnamed x42, local copies, waits for them, and re-layouts: 6.45 us -> 8.09 us
  transfers between devices with their start and end apart: 19 -> 19, of which waited for: 8 -> 6; matrix products, arithmetic and copies ran while one was open for 0% -> 0% of each run, Pallas kernels for 35% -> 37%
where the time goes in v2:
time: 159 us
  Pallas kernels  74.3 us (47%)
  starting transfers between devices  50.9 us (32%)
  waiting for transfers between devices  24.3 us (15%)
  local copies, waits for them, and re-layouts  8.21 us (5%)
    ppermute x8, starting transfers between devices, from_above(): return lax.ppermute(value, 'tensor', above)  20.8 us
    pallas_call x2, Pallas kernels, turn(): call(turn_body, struct((SIDES, WID, PAD)), grid=(3,), in_specs=[sm(), pl....  13.3 us
    pallas_call x1, Pallas kernels, shards(): call(back_body, (mid, mid, struct((ROWS, 128), F32), half, half), in_spec...  11.8 us
    ppermute x8, waiting for transfers between devices, from_above(): return lax.ppermute(value, 'tensor', above)  11.6 us
    all_to_all x1, starting transfers between devices, shards(): back = lax.all_to_all(send_back, 'dp', 0, 0, tiled=True)  10.4 us
    pallas_call x1, Pallas kernels, shards(): call(grad_pair_body, (struct((WID, FEAT)), struct((WID, FEAT))), grid=(3,...  9.75 us
    all_to_all x1, starting transfers between devices, shards(): got_x = lax.all_to_all(send_x, 'dp', 0, 0, tiled=True)  9.45 us
    pallas_call x1, Pallas kernels, shards(): call(gate_up_near_body, (struct((2, ROWS, PAD), F32), struct((SIDES, ROWS...  9.2 us
  transfers between devices with their start and end apart: 19, of which 6 were waited for; matrix products, arithmetic and copies ran while one was open for 0% of the time, Pallas kernels for 37%

profile of v2, /device:TPU:1, one launch (start us, length us, event | category | flops | bytes accessed | tf_op | source)
XLA Modules:
  0.0 158.6 jit_solution(1426004531928017789)
XLA Ops:
  0.6 2.1 %collective-permute-start = (bf16[720,384]{1,0:T(8,128)(2,1)}, bf16[720,384]{1,0:T(8,128)(2,1)S(1)}, u32[]{:S(2)}, u32[]{:S(2)}) collective-permute-start(bf16[720,384]{1,0:T(8,128)(2,1)} %bitcast.24), channel_id=1, source_target_pairs={{3,0},{0,1},{1,2},{2,3},{7,4},{4,5},{5,6},{6,7},{11,8},{8,9},{9,10... | collective-permute-start | bytes 1658888 | tf_op jit(solution)/shard_map/ppermute | solution.py:471
  2.7 1.3 collective-permute-start.1
  4.1 3.3 %shard_map.119 = (bf16[32,112,128]{2,1,0:T(8,128)(2,1)}, bf16[576,384]{1,0:T(8,128)(2,1)}) custom-call(s32[4,384]{1,0:T(4,128)} %bitcast.27, bf16[4,384]{1,0:T(4,128)(2,1)} %bitcast.35, s32[1,128]{1,0:T(1,128)} %bitcast.29, bf16[720,384]{1,0:T(8,128)(2,1)} %bitcast.34), custom_call_target="tpu_custom_call" | custom-call | flops 1000000000 | bytes 4194304 | tf_op jit(solution)/shard_map/pallas_call | solution.py:481
  7.4 9.4 %all-to-all-start.1 = ((bf16[32,112,128]{2,1,0:T(8,128)(2,1)}), bf16[32,112,128]{2,1,0:T(8,128)(2,1)S(1)}, u32[]{:S(2)}, u32[]{:S(2)}) async-start(bf16[32,112,128]{2,1,0:T(8,128)(2,1)} %get-tuple-element.36), calls=%async_computation.1 | async-start | bytes 1835008 | tf_op jit(solution)/shard_map/all_to_all | solution.py:490
  16.9 0.1 collective-permute-start.2
  17.1 2.7 %collective-permute-start.3 = (bf16[352,384]{1,0:T(8,128)(2,1)S(1)}, bf16[352,384]{1,0:T(8,128)(2,1)S(1)}, u32[]{:S(2)}, u32[]{:S(2)}) collective-permute-start(bf16[352,384]{1,0:T(8,128)(2,1)S(1)} %slice.17), channel_id=1, source_target_pairs={{1,0},{2,1},{3,2},{0,3},{5,4},{6,5},{7,6},{4,7},{9,8},{10,9},{11,1... | collective-permute-start | bytes 811016 | tf_op jit(solution)/shard_map/ppermute | solution.py:468
  19.8 4.7 %collective-permute-done.3.far_b_ref = bf16[352,384]{1,0:T(8,128)(2,1)S(1)} collective-permute-done((bf16[352,384]{1,0:T(8,128)(2,1)S(1)}, bf16[352,384]{1,0:T(8,128)(2,1)S(1)}, u32[]{:S(2)}, u32[]{:S(2)}) %collective-permute-start.3) | collective-permute-done | bytes 270368 | tf_op jit(solution)/shard_map/ppermute | solution.py:468
  24.5 1.2 collective-permute-done.2.far_a_ref
  25.7 1.0 copy-done.10
  26.7 4.1 %shard_map.120 = bf16[32,416,128]{2,1,0:T(8,128)(2,1)} custom-call(s32[1]{0:T(128)} %bitcast.t_ref, bf16[576,384]{1,0:T(8,128)(2,1)S(1)} %copy-done.10, bf16[720,384]{1,0:T(8,128)(2,1)S(1)} %bitcast.26, bf16[720,384]{1,0:T(8,128)(2,1)S(1)} %collective-permute-done.below_ref, bf16[720,384]{1,0:T(8,128)(2,1)S(1)} %collective-permute-done.1.above_ref, ...), custom_call_target="tpu_custom_call" | custom-call | flops 2000000000 | bytes 4194304 | tf_op jit(solution)/shard_map/pallas_call | solution.py:497
  30.8 1.7 %all-to-all-done.1.refs_0_ = bf16[32,112,128]{2,1,0:T(8,128)(2,1)S(1)} async-done(((bf16[32,112,128]{2,1,0:T(8,128)(2,1)}), bf16[32,112,128]{2,1,0:T(8,128)(2,1)S(1)}, u32[]{:S(2)}, u32[]{:S(2)}) %all-to-all-start.1) | async-done | bytes 917536 | tf_op jit(solution)/shard_map/all_to_all | solution.py:490
  32.5 7.6 %all-to-all-start = ((bf16[32,416,128]{2,1,0:T(8,128)(2,1)}), bf16[32,416,128]{2,1,0:T(8,128)(2,1)}, u32[]{:S(2)}, u32[]{:S(2)}) async-start(bf16[32,416,128]{2,1,0:T(8,128)(2,1)} %shard_map.120), calls=%async_computation | async-start | bytes 6815744 | tf_op jit(solution)/shard_map/all_to_all | solution.py:506
  40.1 0.1 fusion
  40.2 2.6 %collective-permute-start.6 = (bf16[16,112,128]{2,1,0:T(8,128)(2,1)S(1)}, bf16[16,112,128]{2,1,0:T(8,128)(2,1)S(1)}, u32[]{:S(2)}, u32[]{:S(2)}) collective-permute-start(bf16[16,112,128]{2,1,0:T(8,128)(2,1)S(1)} %get-tuple-element.61), channel_id=1, source_target_pairs={{1,0},{2,1},{3,2},{0,3},{5,4},{6,5},{7,6},{4,7},{9,8},{10,9},{11,1... | collective-permute-start | bytes 1376264 | tf_op jit(solution)/shard_map/ppermute | solution.py:468
  42.8 2.7 %collective-permute-start.9 = (bf16[16,112,128]{2,1,0:T(8,128)(2,1)S(1)}, bf16[16,112,128]{2,1,0:T(8,128)(2,1)S(1)}, u32[]{:S(2)}, u32[]{:S(2)}) collective-permute-start(bf16[16,112,128]{2,1,0:T(8,128)(2,1)S(1)} %get-tuple-element.62), channel_id=1, source_target_pairs={{1,0},{2,1},{3,2},{0,3},{5,4},{6,5},{7,6},{4,7},{9,8},{10,9},{11,1... | collective-permute-start | bytes 1376264 | tf_op jit(solution)/shard_map/ppermute | solution.py:468
  45.5 6.9 %collective-permute-done.6.refs_4_ = bf16[16,112,128]{2,1,0:T(8,128)(2,1)S(1)} collective-permute-done((bf16[16,112,128]{2,1,0:T(8,128)(2,1)S(1)}, bf16[16,112,128]{2,1,0:T(8,128)(2,1)S(1)}, u32[]{:S(2)}, u32[]{:S(2)}) %collective-permute-start.6) | collective-permute-done | bytes 458784 | tf_op jit(solution)/shard_map/ppermute | solution.py:468
  52.4 3.5 %collective-permute-start.7 = (bf16[16,112,128]{2,1,0:T(8,128)(2,1)S(1)}, bf16[16,112,128]{2,1,0:T(8,128)(2,1)S(1)}, u32[]{:S(2)}, u32[]{:S(2)}) collective-permute-start(bf16[16,112,128]{2,1,0:T(8,128)(2,1)S(1)} %collective-permute-done.6.refs_4_), channel_id=1, source_target_pairs={{1,0},{2,1},{3,2},{0,3},{5,4},{6,5},{7,6},{4,7},{9,8},{10,9},{11,1... | collective-permute-start | bytes 1376264 | tf_op jit(solution)/shard_map/ppermute | solution.py:468
  55.9 6.7 %shard_map.122.refs_6_.refs_4_.wu_hbm.wu_ref.wua_ref.wub_ref = bf16[4,720,768]{2,1,0:T(8,128)(2,1)} custom-call(s32[1]{0:T(128)} %bitcast.t_ref, bf16[720,2880]{1,0:T(8,128)(2,1)} %bitcast.31), custom_call_target="tpu_custom_call" | custom-call | bytes 4194304 | tf_op jit(solution)/shard_map/pallas_call | solution.py:437
  62.6 6.6 %shard_map.121.refs_5_.refs_3_.wg_hbm.wg_ref.wga_ref.wgb_ref = bf16[4,720,768]{2,1,0:T(8,128)(2,1)} custom-call(s32[1]{0:T(128)} %bitcast.t_ref, bf16[720,2880]{1,0:T(8,128)(2,1)} %bitcast.32), custom_call_target="tpu_custom_call" | custom-call | bytes 4194304 | tf_op jit(solution)/shard_map/pallas_call | solution.py:437
  69.2 0.8 copy-done.17
  70.0 0.8 copy-done.18
  70.7 9.2 %shard_map.123 = (f32[2,576,768]{2,1,0:T(8,128)}, bf16[4,576,768]{2,1,0:T(8,128)(2,1)}) custom-call(bf16[32,112,128]{2,1,0:T(8,128)(2,1)} %copy-done.12, bf16[16,112,128]{2,1,0:T(8,128)(2,1)} %copy-done.16, bf16[16,112,128]{2,1,0:T(8,128)(2,1)} %copy-done.17, bf16[16,112,128]{2,1,0:T(8,128)(2,1)} %copy-done.18, bf16[16,112,128]{2,1,0:T(8,128)(2,1)} %copy-done.15, ...), custom_call_target="tpu_custom_call" | custom-call | flops 4000000000 | bytes 4194304 | tf_op jit(solution)/shard_map/pallas_call | solution.py:512
  80.0 0.0 copy-start.14
  80.0 0.7 copy-done.13
  80.7 0.1 copy-done.14
  80.9 6.5 %shard_map.124 = (bf16[576,768]{1,0:T(8,128)(2,1)}, bf16[2,576,768]{2,1,0:T(8,128)(2,1)}, bf16[4,576,768]{2,1,0:T(8,128)(2,1)}) custom-call(bf16[16,112,128]{2,1,0:T(8,128)(2,1)} %copy-done.14, bf16[16,112,128]{2,1,0:T(8,128)(2,1)} %copy-done.13, f32[2,576,768]{2,1,0:T(8,128)} %get-tuple-element.37.refs_2_, ...), custom_call_target="tpu_custom_call", output_to_operand_aliasing={{2}: (5, {})} | custom-call | flops 1500000000 | bytes 4194304 | tf_op jit(solution)/shard_map/pallas_call | solution.py:529
  87.3 11.8 %shard_map.125 = (bf16[576,768]{1,0:T(8,128)(2,1)}, bf16[576,768]{1,0:T(8,128)(2,1)}, f32[576,128]{1,0:T(8,128)S(1)}, bf16[288,768]{1,0:T(8,128)(2,1)S(1)}, bf16[288,768]{1,0:T(8,128)(2,1)S(1)}) custom-call(bf16[32,416,128]{2,1,0:T(8,128)(2,1)} %all-to-all-done.got_hbm.got, bf16[720,2880]{1,0:T(8,128)(2,1)} %bitcast.33, ...), custom_call_target="tpu_custom_call" | custom-call | flops 4000000000 | bytes 4194304 | tf_op jit(solution)/shard_map/pallas_call | solution.py:549
  99.1 0.3 collective-permute-start.10
  99.4 2.7 %collective-permute-start.11 = (bf16[288,768]{1,0:T(8,128)(2,1)S(1)}, bf16[288,768]{1,0:T(8,128)(2,1)S(1)}, u32[]{:S(2)}, u32[]{:S(2)}) collective-permute-start(bf16[288,768]{1,0:T(8,128)(2,1)S(1)} %get-tuple-element.47), channel_id=1, source_target_pairs={{1,0},{2,1},{3,2},{0,3},{5,4},{6,5},{7,6},{4,7},{9,8},{10,9},{11,1... | collective-permute-start | bytes 1327112 | tf_op jit(solution)/shard_map/ppermute | solution.py:468
  102.1 2.3 %copy-done = bf16[4,720,768]{2,1,0:T(8,128)(2,1)S(1)} copy-done((bf16[4,720,768]{2,1,0:T(8,128)(2,1)S(1)}, bf16[4,720,768]{2,1,0:T(8,128)(2,1)}, u32[]{:S(2)}) %copy-start) | copy-done | bytes 4423704
  104.3 1.2 copy-done.1
  105.5 1.2 copy-done.3
  106.7 2.9 %shard_map.127 = (bf16[288,768]{1,0:T(8,128)(2,1)S(1)}, bf16[288,768]{1,0:T(8,128)(2,1)S(1)}, f32[288,768]{1,0:T(8,128)S(1)}, f32[288,768]{1,0:T(8,128)S(1)}) custom-call(bf16[576,768]{1,0:T(8,128)(2,1)S(1)} %copy-done.1, bf16[576,768]{1,0:T(8,128)(2,1)S(1)} %copy-done.3, bf16[4,720,768]{2,1,0:T(8,128)(2,1)S(1)} %copy-done, ...), custom_call_target="tpu_custom_call" | custom-call | flops 2400000000 | bytes 4194304 | tf_op jit(solution)/shard_map/pallas_call | solution.py:573
  109.6 0.1 collective-permute-start.14
  109.7 0.0 copy-start.5
  109.7 2.6 %collective-permute-start.15 = (bf16[288,768]{1,0:T(8,128)(2,1)S(1)}, bf16[288,768]{1,0:T(8,128)(2,1)S(1)}, u32[]{:S(2)}, u32[]{:S(2)}) collective-permute-start(bf16[288,768]{1,0:T(8,128)(2,1)S(1)} %get-tuple-element.55), channel_id=1, source_target_pairs={{1,0},{2,1},{3,2},{0,3},{5,4},{6,5},{7,6},{4,7},{9,8},{10,9},{11,1... | collective-permute-start | bytes 1327112 | tf_op jit(solution)/shard_map/ppermute | solution.py:468
  112.4 1.5 shard_map.126.own_ref
  113.9 0.5 shard_map.128
  114.4 0.1 collective-permute-start.12
  114.5 2.7 %collective-permute-start.13 = (bf16[288,768]{1,0:T(8,128)(2,1)S(1)}, bf16[288,768]{1,0:T(8,128)(2,1)S(1)}, u32[]{:S(2)}, u32[]{:S(2)}) collective-permute-start(bf16[288,768]{1,0:T(8,128)(2,1)S(1)} %get-tuple-element.49), channel_id=1, source_target_pairs={{1,0},{2,1},{3,2},{0,3},{5,4},{6,5},{7,6},{4,7},{9,8},{10,9},{11,1... | collective-permute-start | bytes 1327112 | tf_op jit(solution)/shard_map/ppermute | solution.py:468
  117.2 9.7 %shard_map.129 = (bf16[720,2880]{1,0:T(8,128)(2,1)}, bf16[720,2880]{1,0:T(8,128)(2,1)}) custom-call(s32[1]{0:T(128)} %bitcast.t_ref, bf16[4,576,768]{2,1,0:T(8,128)(2,1)S(1)} %copy-done.5, bf16[576,768]{1,0:T(8,128)(2,1)S(1)} %copy-done.2, bf16[576,768]{1,0:T(8,128)(2,1)S(1)} %copy-done.4), custom_call_target="tpu_custom_call" | custom-call | flops 5000000000 | bytes 4194304 | tf_op jit(solution)/shard_map/pallas_call | solution.py:596
  127.0 2.5 %collective-permute-done.12.below_a = bf16[288,768]{1,0:T(8,128)(2,1)S(1)} collective-permute-done((bf16[288,768]{1,0:T(8,128)(2,1)S(1)}, bf16[288,768]{1,0:T(8,128)(2,1)S(1)}, u32[]{:S(2)}, u32[]{:S(2)}) %collective-permute-start.12) | collective-permute-done | bytes 442400 | tf_op jit(solution)/shard_map/ppermute | solution.py:471
  129.5 1.4 shard_map.130
  130.9 10.4 %all-to-all-start.2 = ((bf16[32,112,128]{2,1,0:T(8,128)(2,1)}), bf16[32,112,128]{2,1,0:T(8,128)(2,1)S(1)}, u32[]{:S(2)}, u32[]{:S(2)}) async-start(bf16[32,112,128]{2,1,0:T(8,128)(2,1)} %shard_map.130), calls=%async_computation.2 | async-start | bytes 1835008 | tf_op jit(solution)/shard_map/all_to_all | solution.py:614
  141.3 0.0 copy-start.8
  141.3 8.4 %shard_map.132 = bf16[720,2880]{1,0:T(8,128)(2,1)} custom-call(bf16[32,416,128]{2,1,0:T(8,128)(2,1)} %all-to-all-done.got_hbm.got, bf16[576,768]{1,0:T(8,128)(2,1)S(1)} %copy-done.6, bf16[576,768]{1,0:T(8,128)(2,1)S(1)} %copy-done.6), custom_call_target="tpu_custom_call" | custom-call | flops 3000000000 | bytes 4194304 | tf_op jit(solution)/shard_map/pallas_call | solution.py:615
  149.7 7.2 %all-to-all-done.2.back_ref = bf16[32,112,128]{2,1,0:T(8,128)(2,1)S(1)} async-done(((bf16[32,112,128]{2,1,0:T(8,128)(2,1)}), bf16[32,112,128]{2,1,0:T(8,128)(2,1)S(1)}, u32[]{:S(2)}, u32[]{:S(2)}) %all-to-all-start.2) | async-done | bytes 917536 | tf_op jit(solution)/shard_map/all_to_all | solution.py:614
  156.9 1.7 %shard_map.131 = (bf16[720,384]{1,0:T(8,128)(2,1)}, bf16[4,384]{1,0:T(4,128)(2,1)}) custom-call(bf16[32,112,128]{2,1,0:T(8,128)(2,1)S(1)} %all-to-all-done.2.back_ref, bf16[576,384]{1,0:T(8,128)(2,1)S(1)} %copy-done.11, s32[4,384]{1,0:T(4,128)S(1)} %bitcast.28, s32[1,128]{1,0:T(1,128)S(1)} %bitcast.30), custom_call_target="tpu_custom_call" | custom-call | flops 1000000000 | bytes 4194304 | tf_op jit(solution)/shard_map/pallas_call | solution.py:625
  (50 shorter events, 0.2 us)
Async XLA Ops:
  0.6 25.0 %copy-start.7 = (bf16[384,720]{0,1:T(8,128)(2,1)S(1)}, bf16[384,720]{0,1:T(8,128)(2,1)}, u32[]{:S(2)}) copy-start(bf16[384,720]{0,1:T(8,128)(2,1)} %param.9) | copy-start | bytes 1658884
  0.6 16.2 %collective-permute-start = (bf16[720,384]{1,0:T(8,128)(2,1)}, bf16[720,384]{1,0:T(8,128)(2,1)S(1)}, u32[]{:S(2)}, u32[]{:S(2)}) collective-permute-start(bf16[720,384]{1,0:T(8,128)(2,1)} %bitcast.24), channel_id=1, source_target_pairs={{3,0},{0,1},{1,2},{2,3},{7,4},{4,5},{5,6},{6,7},{11,8},{8,9},{9,10... | collective-permute-start | bytes 1658888 | tf_op jit(solution)/shard_map/ppermute | solution.py:471
  2.7 14.3 %collective-permute-start.1 = (bf16[720,384]{1,0:T(8,128)(2,1)}, bf16[720,384]{1,0:T(8,128)(2,1)S(1)}, u32[]{:S(2)}, u32[]{:S(2)}) collective-permute-start(bf16[720,384]{1,0:T(8,128)(2,1)} %bitcast.25), channel_id=1, source_target_pairs={{1,0},{2,1},{3,2},{0,3},{5,4},{6,5},{7,6},{4,7},{9,8},{10,9},{11,1... | collective-permute-start | bytes 1658888 | tf_op jit(solution)/shard_map/ppermute | solution.py:468
  7.4 25.1 %all-to-all-start.1 = ((bf16[32,112,128]{2,1,0:T(8,128)(2,1)}), bf16[32,112,128]{2,1,0:T(8,128)(2,1)S(1)}, u32[]{:S(2)}, u32[]{:S(2)}) async-start(bf16[32,112,128]{2,1,0:T(8,128)(2,1)} %get-tuple-element.36), calls=%async_computation.1 | async-start | bytes 1835008 | tf_op jit(solution)/shard_map/all_to_all | solution.py:490
  16.9 8.8 %collective-permute-start.2 = (bf16[368,384]{1,0:T(8,128)(2,1)S(1)}, bf16[368,384]{1,0:T(8,128)(2,1)S(1)}, u32[]{:S(2)}, u32[]{:S(2)}) collective-permute-start(bf16[368,384]{1,0:T(8,128)(2,1)S(1)} %slice.16), channel_id=1, source_target_pairs={{3,0},{0,1},{1,2},{2,3},{7,4},{4,5},{5,6},{6,7},{11,8},{8,9},{9,10... | collective-permute-start | bytes 847880 | tf_op jit(solution)/shard_map/ppermute | solution.py:471
  17.1 7.5 %collective-permute-start.3 = (bf16[352,384]{1,0:T(8,128)(2,1)S(1)}, bf16[352,384]{1,0:T(8,128)(2,1)S(1)}, u32[]{:S(2)}, u32[]{:S(2)}) collective-permute-start(bf16[352,384]{1,0:T(8,128)(2,1)S(1)} %slice.17), channel_id=1, source_target_pairs={{1,0},{2,1},{3,2},{0,3},{5,4},{6,5},{7,6},{4,7},{9,8},{10,9},{11,1... | collective-permute-start | bytes 811016 | tf_op jit(solution)/shard_map/ppermute | solution.py:468
  25.7 1.0 copy-start.10
  32.5 7.7 %copy-start.12 = (bf16[32,112,128]{2,1,0:T(8,128)(2,1)}, bf16[32,112,128]{2,1,0:T(8,128)(2,1)S(1)}, u32[]{:S(2)}) copy-start(bf16[32,112,128]{2,1,0:T(8,128)(2,1)S(1)} %all-to-all-done.1.refs_0_) | copy-start | bytes 2752516
  32.5 54.8 %all-to-all-start = ((bf16[32,416,128]{2,1,0:T(8,128)(2,1)}), bf16[32,416,128]{2,1,0:T(8,128)(2,1)}, u32[]{:S(2)}, u32[]{:S(2)}) async-start(bf16[32,416,128]{2,1,0:T(8,128)(2,1)} %shard_map.120), calls=%async_computation | async-start | bytes 6815744 | tf_op jit(solution)/shard_map/all_to_all | solution.py:506
  40.2 12.2 %collective-permute-start.6 = (bf16[16,112,128]{2,1,0:T(8,128)(2,1)S(1)}, bf16[16,112,128]{2,1,0:T(8,128)(2,1)S(1)}, u32[]{:S(2)}, u32[]{:S(2)}) collective-permute-start(bf16[16,112,128]{2,1,0:T(8,128)(2,1)S(1)} %get-tuple-element.61), channel_id=1, source_target_pairs={{1,0},{2,1},{3,2},{0,3},{5,4},{6,5},{7,6},{4,7},{9,8},{10,9},{11,1... | collective-permute-start | bytes 1376264 | tf_op jit(solution)/shard_map/ppermute | solution.py:468
  42.8 13.1 %collective-permute-start.4 = (bf16[16,112,128]{2,1,0:T(8,128)(2,1)S(1)}, bf16[16,112,128]{2,1,0:T(8,128)(2,1)S(1)}, u32[]{:S(2)}, u32[]{:S(2)}) collective-permute-start(bf16[16,112,128]{2,1,0:T(8,128)(2,1)S(1)} %get-tuple-element.62), channel_id=1, source_target_pairs={{3,0},{0,1},{1,2},{2,3},{7,4},{4,5},{5,6},{6,7},{11,8},{8,9},{9,10... | collective-permute-start | bytes 1376264 | tf_op jit(solution)/shard_map/ppermute | solution.py:471
  42.8 26.4 %collective-permute-start.8 = (bf16[16,112,128]{2,1,0:T(8,128)(2,1)S(1)}, bf16[16,112,128]{2,1,0:T(8,128)(2,1)S(1)}, u32[]{:S(2)}, u32[]{:S(2)}) collective-permute-start(bf16[16,112,128]{2,1,0:T(8,128)(2,1)S(1)} %get-tuple-element.61), channel_id=1, source_target_pairs={{3,0},{0,1},{1,2},{2,3},{7,4},{4,5},{5,6},{6,7},{11,8},{8,9},{9,10... | collective-permute-start | bytes 1376264 | tf_op jit(solution)/shard_map/ppermute | solution.py:471
  42.8 26.4 %collective-permute-start.9 = (bf16[16,112,128]{2,1,0:T(8,128)(2,1)S(1)}, bf16[16,112,128]{2,1,0:T(8,128)(2,1)S(1)}, u32[]{:S(2)}, u32[]{:S(2)}) collective-permute-start(bf16[16,112,128]{2,1,0:T(8,128)(2,1)S(1)} %get-tuple-element.62), channel_id=1, source_target_pairs={{1,0},{2,1},{3,2},{0,3},{5,4},{6,5},{7,6},{4,7},{9,8},{10,9},{11,1... | collective-permute-start | bytes 1376264 | tf_op jit(solution)/shard_map/ppermute | solution.py:468
  52.4 10.3 %copy-start.15 = (bf16[16,112,128]{2,1,0:T(8,128)(2,1)}, bf16[16,112,128]{2,1,0:T(8,128)(2,1)S(1)}, u32[]{:S(2)}) copy-start(bf16[16,112,128]{2,1,0:T(8,128)(2,1)S(1)} %collective-permute-done.6.refs_4_) | copy-start | bytes 1376260
  52.4 27.6 %collective-permute-start.7 = (bf16[16,112,128]{2,1,0:T(8,128)(2,1)S(1)}, bf16[16,112,128]{2,1,0:T(8,128)(2,1)S(1)}, u32[]{:S(2)}, u32[]{:S(2)}) collective-permute-start(bf16[16,112,128]{2,1,0:T(8,128)(2,1)S(1)} %collective-permute-done.6.refs_4_), channel_id=1, source_target_pairs={{1,0},{2,1},{3,2},{0,3},{5,4},{6,5},{7,6},{4,7},{9,8},{10,9},{11,1... | collective-permute-start | bytes 1376264 | tf_op jit(solution)/shard_map/ppermute | solution.py:468
  55.9 6.7 %copy-start.16 = (bf16[16,112,128]{2,1,0:T(8,128)(2,1)}, bf16[16,112,128]{2,1,0:T(8,128)(2,1)S(1)}, u32[]{:S(2)}) copy-start(bf16[16,112,128]{2,1,0:T(8,128)(2,1)S(1)} %collective-permute-done.4.refs_1_) | copy-start | bytes 1376260
  55.9 24.1 %collective-permute-start.5 = (bf16[16,112,128]{2,1,0:T(8,128)(2,1)S(1)}, bf16[16,112,128]{2,1,0:T(8,128)(2,1)S(1)}, u32[]{:S(2)}, u32[]{:S(2)}) collective-permute-start(bf16[16,112,128]{2,1,0:T(8,128)(2,1)S(1)} %collective-permute-done.4.refs_1_), channel_id=1, source_target_pairs={{3,0},{0,1},{1,2},{2,3},{7,4},{4,5},{5,6},{6,7},{11,8},{8,9},{9,10... | collective-permute-start | bytes 1376264 | tf_op jit(solution)/shard_map/ppermute | solution.py:471
  69.2 0.8 copy-start.17
  70.0 0.8 copy-start.18
  79.9 0.8 copy-start.13
  80.0 0.9 copy-start.14
  80.9 21.2 %slice-start = ((s8[4423680]{0:T(1024)(128)(4,1)}), s8[229376]{0:T(1024)(128)(4,1)S(1)}, s32[]{:S(2)}) async-start(s8[4423680]{0:T(1024)(128)(4,1)} %bitcast.22), calls=%async_computation.3 | async-start | bytes 458752
  87.3 14.8 %slice-start.1 = ((s8[4423680]{0:T(1024)(128)(4,1)}), s8[4194304]{0:T(1024)(128)(4,1)S(1)}, s32[]{:S(2)}) async-start(s8[4423680]{0:T(1024)(128)(4,1)} %bitcast.22), calls=%async_computation.4 | async-start | bytes 8388608
  99.1 14.8 %collective-permute-start.10 = (bf16[288,768]{1,0:T(8,128)(2,1)S(1)}, bf16[288,768]{1,0:T(8,128)(2,1)S(1)}, u32[]{:S(2)}, u32[]{:S(2)}) collective-permute-start(bf16[288,768]{1,0:T(8,128)(2,1)S(1)} %get-tuple-element.45), channel_id=1, source_target_pairs={{3,0},{0,1},{1,2},{2,3},{7,4},{4,5},{5,6},{6,7},{11,8},{8,9},{9,10... | collective-permute-start | bytes 1327112 | tf_op jit(solution)/shard_map/ppermute | solution.py:471
  99.4 14.5 %collective-permute-start.11 = (bf16[288,768]{1,0:T(8,128)(2,1)S(1)}, bf16[288,768]{1,0:T(8,128)(2,1)S(1)}, u32[]{:S(2)}, u32[]{:S(2)}) collective-permute-start(bf16[288,768]{1,0:T(8,128)(2,1)S(1)} %get-tuple-element.47), channel_id=1, source_target_pairs={{1,0},{2,1},{3,2},{0,3},{5,4},{6,5},{7,6},{4,7},{9,8},{10,9},{11,1... | collective-permute-start | bytes 1327112 | tf_op jit(solution)/shard_map/ppermute | solution.py:468
  102.1 2.3 %copy-start = (bf16[4,720,768]{2,1,0:T(8,128)(2,1)S(1)}, bf16[4,720,768]{2,1,0:T(8,128)(2,1)}, u32[]{:S(2)}) copy-start(bf16[4,720,768]{2,1,0:T(8,128)(2,1)} %shard_map.121.refs_5_.refs_3_.wg_hbm.wg_ref.wga_ref.wgb_ref) | copy-start | bytes 13271044
  104.3 1.2 copy-start.1
  105.5 1.2 copy-start.3
  106.7 5.7 %copy-start.4 = (bf16[576,768]{1,0:T(8,128)(2,1)S(1)}, bf16[576,768]{1,0:T(8,128)(2,1)}, u32[]{:S(2)}) copy-start(bf16[576,768]{1,0:T(8,128)(2,1)} %get-tuple-element.42.gu_ref) | copy-start | bytes 2654212
  109.6 19.8 %collective-permute-start.14 = (bf16[288,768]{1,0:T(8,128)(2,1)S(1)}, bf16[288,768]{1,0:T(8,128)(2,1)S(1)}, u32[]{:S(2)}, u32[]{:S(2)}) collective-permute-start(bf16[288,768]{1,0:T(8,128)(2,1)S(1)} %get-tuple-element.54), channel_id=1, source_target_pairs={{3,0},{0,1},{1,2},{2,3},{7,4},{4,5},{5,6},{6,7},{11,8},{8,9},{9,10... | collective-permute-start | bytes 1327112 | tf_op jit(solution)/shard_map/ppermute | solution.py:471
  109.7 7.5 %copy-start.2 = (bf16[576,768]{1,0:T(8,128)(2,1)S(1)}, bf16[576,768]{1,0:T(8,128)(2,1)}, u32[]{:S(2)}) copy-start(bf16[576,768]{1,0:T(8,128)(2,1)} %get-tuple-element.41.gg_ref) | copy-start | bytes 2654212
  109.7 7.5 %copy-start.5 = (bf16[4,576,768]{2,1,0:T(8,128)(2,1)S(1)}, bf16[4,576,768]{2,1,0:T(8,128)(2,1)}, u32[]{:S(2)}) copy-start(bf16[4,576,768]{2,1,0:T(8,128)(2,1)} %get-tuple-element.50.x_ref) | copy-start | bytes 10616836
  109.7 19.7 %collective-permute-start.15 = (bf16[288,768]{1,0:T(8,128)(2,1)S(1)}, bf16[288,768]{1,0:T(8,128)(2,1)S(1)}, u32[]{:S(2)}, u32[]{:S(2)}) collective-permute-start(bf16[288,768]{1,0:T(8,128)(2,1)S(1)} %get-tuple-element.55), channel_id=1, source_target_pairs={{1,0},{2,1},{3,2},{0,3},{5,4},{6,5},{7,6},{4,7},{9,8},{10,9},{11,1... | collective-permute-start | bytes 1327112 | tf_op jit(solution)/shard_map/ppermute | solution.py:468
  114.4 15.0 %collective-permute-start.12 = (bf16[288,768]{1,0:T(8,128)(2,1)S(1)}, bf16[288,768]{1,0:T(8,128)(2,1)S(1)}, u32[]{:S(2)}, u32[]{:S(2)}) collective-permute-start(bf16[288,768]{1,0:T(8,128)(2,1)S(1)} %get-tuple-element.48), channel_id=1, source_target_pairs={{3,0},{0,1},{1,2},{2,3},{7,4},{4,5},{5,6},{6,7},{11,8},{8,9},{9,10... | collective-permute-start | bytes 1327112 | tf_op jit(solution)/shard_map/ppermute | solution.py:471
  114.5 14.9 %collective-permute-start.13 = (bf16[288,768]{1,0:T(8,128)(2,1)S(1)}, bf16[288,768]{1,0:T(8,128)(2,1)S(1)}, u32[]{:S(2)}, u32[]{:S(2)}) collective-permute-start(bf16[288,768]{1,0:T(8,128)(2,1)S(1)} %get-tuple-element.49), channel_id=1, source_target_pairs={{1,0},{2,1},{3,2},{0,3},{5,4},{6,5},{7,6},{4,7},{9,8},{10,9},{11,1... | collective-permute-start | bytes 1327112 | tf_op jit(solution)/shard_map/ppermute | solution.py:468
  126.9 14.3 %copy-start.6 = (bf16[576,768]{1,0:T(8,128)(2,1)S(1)}, bf16[576,768]{1,0:T(8,128)(2,1)}, u32[]{:S(2)}) copy-start(bf16[576,768]{1,0:T(8,128)(2,1)} %get-tuple-element.39.act_hbm.act_ref.act_tail_ref) | copy-start | bytes 2654212
  130.9 26.1 %all-to-all-start.2 = ((bf16[32,112,128]{2,1,0:T(8,128)(2,1)}), bf16[32,112,128]{2,1,0:T(8,128)(2,1)S(1)}, u32[]{:S(2)}, u32[]{:S(2)}) async-start(bf16[32,112,128]{2,1,0:T(8,128)(2,1)} %shard_map.130), calls=%async_computation.2 | async-start | bytes 1835008 | tf_op jit(solution)/shard_map/all_to_all | solution.py:614
  141.3 15.6 %copy-start.8 = (s32[384,4]{0,1:T(4,128)S(1)}, s32[384,4]{0,1:T(4,128)}, u32[]{:S(2)}) copy-start(s32[384,4]{0,1:T(4,128)} %param.11) | copy-start | bytes 18436
  141.3 15.6 %copy-start.9 = (s32[128]{0:T(128)S(1)}, s32[128]{0:T(128)}, u32[]{:S(2)}) copy-start(s32[128]{0:T(128)} %param.12) | copy-start | bytes 1540
  141.3 15.6 %copy-start.11 = (bf16[576,384]{1,0:T(8,128)(2,1)S(1)}, bf16[576,384]{1,0:T(8,128)(2,1)}, u32[]{:S(2)}) copy-start(bf16[576,384]{1,0:T(8,128)(2,1)} %get-tuple-element.34.pick_ref) | copy-start | bytes 1327108
